TPU v7x, 256 devices: a whole 4x4x8 slice. The times are simulated.
256 devices in a mesh: dp: 64 (over y, z, core), outer: 4 (over x).
Axes of the slice: x: 4, y: 4, z: 8, core: 2. Of those that a mesh axis runs over, the one named last changes fastest.
Arguments:
- clean: bfloat16 [2048, 112, 1024], P(('dp', 'outer')), may hold values from -3 to 3
- noise: bfloat16 [2048, 112, 1024], P(('dp', 'outer')), may hold values from -6 to 6
- t_index: int32 [2048], P(('dp', 'outer')), may hold values from 0 to 1278
- bucket_id: int32 [2048], P(('dp', 'outer')), may hold values from 0 to 15
- bucket_count: int32 [16], replicated, may hold values from 1 to 999
- w_first: bfloat16 [1024, 1024], replicated, may hold values from -0.5 to 0.5
- w_second: bfloat16 [1024, 1024], replicated, may hold values from -0.5 to 0.5
- teacher_first: bfloat16 [1024, 1024], replicated, may hold values from -0.5 to 0.5
- teacher_second: bfloat16 [1024, 1024], replicated, may hold values from -0.5 to 0.5
Outputs:
- grad_first: float32 [1024, 1024], P(('dp', 'outer'))
- grad_second: float32 [1024, 1024], P(('dp', 'outer'))
- bucket_loss: float32 [16], replicated
All inputs are finite; a program needn't handle non-finite values.
Results may differ from a plain program's by a relative error of at most 0.0033.
Values sent between devices are 32-bit elements; how exact they have to be, the bound alone decides.
No kernel may reach another device: no remote copies, remote signals or barrier semaphores. Data moves between devices by JAX's collectives and lax.ppermute only.
A program may use at most 128 MiB of HBM per device.

v0:
```python
import functools, math
import jax, jax.numpy as jnp
from jax import lax
from jax.experimental import pallas as pl
from jax.experimental.pallas import tpu as pltpu
from jax.sharding import Mesh
from jax.sharding import PartitionSpec as P

DP_OUTER = ("dp_0", "dp_1", "dp_2", "outer")

STEPS = 1280
sigma_floor = 0.002
sigma_ceiling = 80.0
sigma_data = 0.5
huber_scale = 0.00054
rho_power = 7.0
F32, BF16 = jnp.float32, jnp.bfloat16
LAT, PATCHES, D, H, BUCKETS = 8, 112, 1024, 1024, 16
ROWS = LAT * PATCHES
TILE = (8, 128)
TN = 256
MB = 448
CORE, FIRST_AT, SECOND_AT = 0, 1, 2
VMEM = pl.BlockSpec(memory_space=pltpu.VMEM)
SMEM = pl.BlockSpec(memory_space=pltpu.SMEM)
ANY = pl.BlockSpec(memory_space=pltpu.HBM)


def rows_from(values):
    row = lax.broadcasted_iota(jnp.int32, TILE, 0)
    out = jnp.full(TILE, values[0])
    for k in range(1, len(values)):
        out = jnp.where(row == k, values[k], out)
    return out


def plan(index):
    ramp = index.astype(F32) / (STEPS - 1)
    top = sigma_ceiling ** (1.0 / rho_power)
    bottom = sigma_floor ** (1.0 / rho_power)
    base = top + ramp * (bottom - top)
    square = base * base
    fourth = square * square
    return fourth * square * base


def scale_factors(s):
    skip = sigma_data**2 / ((s - sigma_floor) ** 2 + sigma_data**2)
    scale = jnp.sqrt(s * s + sigma_data**2)
    return skip, (s - sigma_floor) * sigma_data / scale, 1.0 / scale


def sigmoid(x):
    return 0.5 * jnp.tanh(0.5 * x) + 0.5


def transposed_dot(a, b):
    return lax.dot_general(a, b, (((0,), (0,)), ((), ())), preferred_element_type=F32)


def store_routed(block, y, t, color, ref):
    v = block.reshape(32, 8, 256)
    left, right = v[:, :, :128], v[:, :, 128:]
    halves = (
        jnp.concatenate([left[:, :4], right[:, :4]], axis=1),
        jnp.concatenate([left[:, 4:], right[:, 4:]], axis=1),
    )
    for x in range(4):
        pieces = halves[x % 2].reshape(8, 2, 2, 8, 128)[:, :, x // 2]
        place = jnp.where(color == 0, x * 4 + y, y * 4 + x)
        for c in range(2):
            ref[pl.ds((place * 2 + t) * 16 + c * 8, 8)] = pieces[:, c]


def weight_gradient(left, right, right_cols, color, ref):
    def part(y, _):
        block = transposed_dot(left[:, pl.ds(pl.multiple_of(y * 256, 256), 256)], right[:, right_cols])
        for t in range(2):
            store_routed(block[:, t * TN:(t + 1) * TN], y, t, color, ref)
        return 0

    lax.fori_loop(0, 4, part, 0, unroll=True)


def half(color):
    return pl.ds(pl.multiple_of(color * 512, 512), 512)


def forward_kernel(place_hbm, t_index_hbm, bucket_id_hbm, bucket_count_hbm, clean_hbm, noise_hbm, w1, w2, t1, t2,
                   send, bucket, grad_out, pre_hi, inputs, act_hi,
                   clean, noise, in_lo, act_lo, diff, coef, wbuf, place, t_index, bucket_id, bucket_count,
                   field_sems, sems, small_sems, *, total):
    small = [pltpu.make_async_copy(src, dst, small_sems.at[k]) for k, (src, dst) in enumerate((
        (place_hbm, place), (t_index_hbm, t_index), (bucket_id_hbm, bucket_id), (bucket_count_hbm, bucket_count)))]
    fields = []
    for lat in range(LAT):
        rows = pl.ds(lat * PATCHES, PATCHES)
        fields.append((pltpu.make_async_copy(clean_hbm.at[lat], clean.at[rows], field_sems.at[0, lat]),
                       pltpu.make_async_copy(noise_hbm.at[lat], noise.at[rows], field_sems.at[1, lat])))
    copies = [pltpu.make_async_copy(src, wbuf.at[k], sems.at[k]) for k, src in enumerate((w1, t1, w2, t2))]
    for copy in small:
        copy.start()
    for pair in fields:
        pair[0].start()
        pair[1].start()
    for copy in copies:
        copy.start()
    for copy in small:
        copy.wait()
    hi_index = rows_from([t_index[k] for k in range(LAT)])
    s_hi, s_lo = plan(hi_index), plan(hi_index + 1)
    skip_hi, out_hi, in_scale_hi = scale_factors(s_hi)
    skip_lo, out_lo, in_scale_lo = scale_factors(s_lo)
    coef[0] = in_scale_hi
    coef[1] = in_scale_lo
    coef[2] = s_hi
    coef[3] = s_lo
    coef[4] = out_hi
    coef[5] = out_lo
    coef[6] = skip_hi
    coef[7] = skip_lo

    def one(k, lat):
        return coef[k, lat:lat + 1, 0:1]

    def block_rows(lat):
        return slice(lat * PATCHES, (lat + 1) * PATCHES)

    def field(lat, side, ref):
        rows = block_rows(lat)
        c, n = clean[rows, :].astype(F32), noise[rows, :].astype(F32)
        ref[rows, :] = (one(side, lat) * (c + one(2 + side, lat) * n)).astype(BF16)

    for lat in range(LAT):
        fields[lat][0].wait()
        fields[lat][1].wait()
        field(lat, 0, inputs)
        field(lat, 1, in_lo)
    copies[0].wait()
    for j in range(H // TN):
        cols = slice(j * TN, (j + 1) * TN)
        pre = jnp.dot(inputs[...], wbuf[0, :, cols], preferred_element_type=F32)
        act_hi[:, cols] = (pre * sigmoid(pre)).astype(BF16)
        pre_hi[:, cols] = pre
    copies[1].wait()
    for j in range(H // TN):
        cols = slice(j * TN, (j + 1) * TN)
        pre = jnp.dot(in_lo[...], wbuf[1, :, cols], preferred_element_type=F32)
        act_lo[:, cols] = (pre * sigmoid(pre)).astype(BF16)
    copies[2].wait()
    copies[3].wait()
    row = lax.broadcasted_iota(jnp.int32, TILE, 0)
    sums = jnp.zeros(TILE, F32)
    for j in range(D // TN):
        cols = slice(j * TN, (j + 1) * TN)
        for m in range(2):
            rows = slice(m * MB, (m + 1) * MB)
            online = jnp.dot(act_hi[rows, :], wbuf[2, :, cols], preferred_element_type=F32)
            target = jnp.dot(act_lo[rows, :], wbuf[3, :, cols], preferred_element_type=F32)
            for k in range(MB // PATCHES):
                lat = m * (MB // PATCHES) + k
                r, s = block_rows(lat), block_rows(k)
                c, n = clean[r, cols].astype(F32), noise[r, cols].astype(F32)
                on = one(6, lat) * (c + one(2, lat) * n) + one(4, lat) * online[s]
                tg = one(7, lat) * (c + one(3, lat) * n) + one(5, lat) * target[s]
                d = on - tg
                diff[r, cols] = d
                sq = jnp.sum((d * d).reshape(PATCHES // 8, 8, TN), axis=0)
                sq = sq[:, :128] + sq[:, 128:]
                sums = sums + jnp.where(row == lat, jnp.sum(sq, axis=0, keepdims=True), 0.0)
    q = jnp.sum(sums, axis=1, keepdims=True)
    c2 = huber_scale * math.sqrt(PATCHES * D)
    root = jnp.sqrt(q + c2**2)
    distance = root - c2
    count = rows_from([bucket_count[bucket_id[k]].astype(F32) for k in range(LAT)])
    weight = s_lo / (s_hi - s_lo) / jnp.sqrt(count) / total
    lane = lax.broadcasted_iota(jnp.int32, TILE, 1)
    part = jnp.where(lane == rows_from([bucket_id[k] for k in range(LAT)]), weight * distance, 0.0)
    bucket[...] = part
    send[512] = part
    coef[8] = out_hi * (weight / root)
    for lat in range(LAT):
        rows = block_rows(lat)
        grad_out[rows, :] = (one(8, lat) * diff[rows, :]).astype(BF16)
    color = 1 - place[CORE]
    weight_gradient(act_hi, grad_out, half(color), color, send)


def second_kernel(info, act_hi, grad_out, keep):
    weight_gradient(act_hi, grad_out, half(info[CORE]), info[CORE], keep)


def first_kernel(info, grad_out, pre_hi, inputs, w2, out, grad_pre, *, color_flip):
    color = 1 - info[CORE] if color_flip else info[CORE]
    cols = half(color)

    def back(m, _):
        rows = pl.ds(pl.multiple_of(m * 224, 224), 224)
        product = lax.dot_general(grad_out[rows, :], w2[cols, :], (((1,), (1,)), ((), ())), preferred_element_type=F32)
        pre = pre_hi[rows, cols]
        sig = sigmoid(pre)
        grad_pre[rows, :] = (product * (sig * (1.0 + pre * (1.0 - sig)))).astype(BF16)
        return 0

    lax.fori_loop(0, 4, back, 0, unroll=True)
    weight_gradient(inputs, grad_pre, slice(None), color, out)


def tiles(n):
    return jax.ShapeDtypeStruct((n, 8, 128), F32)


PRODUCT = 2 * ROWS * D * H


def forward(info, t_index, bucket_id, bucket_count, clean, noise, w1, w2, t1, t2, total):
    return pl.pallas_call(
        functools.partial(forward_kernel, total=total),
        out_shape=(pltpu.VMEM((513, 8, 128), F32), pltpu.VMEM(TILE, F32), pltpu.VMEM((ROWS, D), BF16),
                   pltpu.VMEM((ROWS, H), F32), pltpu.VMEM((ROWS, D), BF16), pltpu.VMEM((ROWS, H), BF16)),
        in_specs=[ANY] * 10,
        out_specs=(VMEM,) * 6,
        scratch_shapes=[pltpu.VMEM((ROWS, D), BF16), pltpu.VMEM((ROWS, D), BF16), pltpu.VMEM((ROWS, D), BF16),
                        pltpu.VMEM((ROWS, H), BF16), pltpu.VMEM((ROWS, D), F32), pltpu.VMEM((9,) + TILE, F32),
                        pltpu.VMEM((4, D, H), BF16), pltpu.SMEM((3,), jnp.int32), pltpu.SMEM((LAT,), jnp.int32),
                        pltpu.SMEM((LAT,), jnp.int32), pltpu.SMEM((BUCKETS,), jnp.int32),
                        pltpu.SemaphoreType.DMA((2, LAT)), pltpu.SemaphoreType.DMA((4,)), pltpu.SemaphoreType.DMA((4,))],
        compiler_params=pltpu.CompilerParams(vmem_limit_bytes=51 * 2**20),
        cost_estimate=pl.CostEstimate(flops=9 * PRODUCT // 2, bytes_accessed=24 * 2**20, transcendentals=2 * ROWS * H),
        name="forward",
    )(info, t_index, bucket_id, bucket_count, clean, noise, w1, w2, t1, t2)


def second_grad(info, act_hi, grad_out):
    return pl.pallas_call(
        second_kernel,
        out_shape=pltpu.VMEM((512, 8, 128), F32),
        in_specs=[SMEM, VMEM, VMEM],
        out_specs=VMEM,
        compiler_params=pltpu.CompilerParams(vmem_limit_bytes=16 * 2**20),
        cost_estimate=pl.CostEstimate(flops=PRODUCT // 2, bytes_accessed=4 * 2**20, transcendentals=0),
        name="second_grad",
    )(info, act_hi, grad_out)


def first_grad(info, grad_out, pre_hi, inputs, w2, color_flip, rows=pltpu.VMEM((512, 8, 128), F32)):
    return pl.pallas_call(
        functools.partial(first_kernel, color_flip=color_flip),
        out_shape=rows,
        in_specs=[SMEM] + [VMEM] * 4,
        out_specs=VMEM,
        scratch_shapes=[pltpu.VMEM((ROWS, 512), BF16)],
        compiler_params=pltpu.CompilerParams(vmem_limit_bytes=20 * 2**20),
        cost_estimate=pl.CostEstimate(flops=PRODUCT, bytes_accessed=8 * 2**20, transcendentals=0),
        name="first_grad",
    )(info, grad_out, pre_hi, inputs, w2)


def call(kernel, outs, ins, vmem_mib, flops, moved):
    return pl.pallas_call(
        kernel,
        out_shape=outs,
        in_specs=[SMEM] + [VMEM] * (len(ins) - 1),
        out_specs=tuple(VMEM for _ in outs),
        compiler_params=pltpu.CompilerParams(vmem_limit_bytes=vmem_mib * 2**20),
        cost_estimate=pl.CostEstimate(flops=flops, bytes_accessed=moved, transcendentals=0),
    )(*ins)


def core_sum_kernel(info, keep, came, *rest, with_bucket):
    bucket, (own, up, down, up_kept, down_kept) = (rest[0], rest[1:]) if with_bucket else (None, rest)

    def half(ref, at, ahead, t):
        p = (info[FIRST_AT] + ahead) % 4
        for q in range(4):
            src = pl.ds(pl.multiple_of(p * 128, 128) + q * 32 + t * 16, 16)
            ref[pl.ds(at + q * 16, 16)] = keep[src] + came[src]

    half(up, 0, 2, 0)
    half(up, 64, 1, 1)
    half(down, 0, 2, 1)
    half(down, 64, 3, 0)
    half(up_kept, 0, 1, 0)
    half(down_kept, 0, 3, 1)
    src = pl.ds(pl.multiple_of(info[FIRST_AT] * 128, 128), 128)
    own[pl.ds(0, 128)] = keep[src] + came[src]
    if with_bucket:
        both = bucket[...] + came[512]
        own[128] = both
        up[128] = both
        down[128] = both
        up_kept[64] = both


def core_sum(info, keep, came, bucket=None):
    more = 0 if bucket is None else 1
    outs = (tiles(128 + more),) * 3 + (tiles(64 + more), tiles(64))
    ins = (info, keep, came) if bucket is None else (info, keep, came, bucket)
    return call(functools.partial(core_sum_kernel, with_bucket=bucket is not None), outs, ins,
                10, 2**19, 6 * 2**20)


def middle_sum_kernel(info, came_up, came_down, up_kept, down_kept, up, down):
    up[pl.ds(0, 64)] = up_kept[pl.ds(0, 64)] + came_up[pl.ds(0, 64)]
    down[...] = down_kept[...] + came_down[pl.ds(0, 64)]
    if up.shape[0] > 64:
        up[64] = up_kept[64] + came_up[128]


def middle_sum(info, came_up, came_down, up_kept, down_kept):
    outs = (tiles(up_kept.shape[0]), tiles(64))
    return call(middle_sum_kernel, outs, (info, came_up, came_down, up_kept, down_kept),
                4, 2**17, 3 * 2**19)


def shift_pairs(k, x_on_core):
    pairs = []
    for y in range(4):
        for z in range(8):
            for core in range(2):
                for x in range(4):
                    to = (y, z, core, (x + k) % 4) if core == x_on_core else ((y + k) % 4, z, core, x)
                    pairs.append((((y * 8 + z) * 2 + core) * 4 + x, ((to[0] * 8 + to[1]) * 2 + to[2]) * 4 + to[3]))
    return pairs


def shift(piece, k, x_on_core):
    return lax.ppermute(piece, DP_OUTER, shift_pairs(k, x_on_core))


def around(info, own, up, down, up_kept, down_kept):
    came_up, came_down = shift(up, 1, 0), shift(down, 3, 0)
    up, down = middle_sum(info, came_up, came_down, up_kept, down_kept)
    up = shift(up, 1, 0)
    down = shift(down, 3, 0)
    return own, came_up, came_down, up, down


def plane_sum_kernel(info, *refs):
    second, first, pieces = refs[:5], refs[5:10], refs[10:]
    for k in range(4):
        q = (info[SECOND_AT] + k) % 4
        for g, (own, came_up, came_down, up, down) in enumerate((second, first)):
            here = pl.multiple_of(q * 32, 32)
            there = pl.multiple_of(q * 16, 16)
            pieces[k][pl.ds(g * 32, 16)] = own[pl.ds(here, 16)] + up[pl.ds(there, 16)] + came_down[pl.ds(64 + there, 16)]
            pieces[k][pl.ds(g * 32 + 16, 16)] = own[pl.ds(here + 16, 16)] + came_up[pl.ds(64 + there, 16)] + down[pl.ds(there, 16)]
        pieces[k][64] = second[0][128] + second[3][64] + second[2][128]


def plane_sum(info, second, first):
    return call(plane_sum_kernel, (tiles(65),) * 4, (info, *second, *first), 10, 2**20, 5 * 2**20)


def exchange(pieces, x_on_core):
    return [pieces[0]] + [shift(pieces[k], k, x_on_core) for k in (1, 3, 2)]


def line_sum_kernel(info, a, b, c, d, out):
    for g in range(2):
        for t in range(2):
            for core in range(2):
                at = pl.ds(g * 32 + t * 16 + core * 8, 8)
                out[:, core, 2 * g + t] = (a[at] + b[at]) + (c[at] + d[at])
    bucket = (a[64] + b[64]) + (c[64] + d[64])
    for z in range(8):
        for core in range(2):
            out[z, core, 4] = bucket


def line_sum(info, pieces):
    outs = (jax.ShapeDtypeStruct((8, 2, 5, 8, 128), F32),)
    return call(line_sum_kernel, outs, (info, *pieces), 4, 2**18, 2**20)[0]


def last_sum_kernel(info, came, first, second, bucket):
    def total(color, at):
        v = [came[2 * z + color, at] for z in range(8)]
        return ((v[0] + v[1]) + (v[2] + v[3])) + ((v[4] + v[5]) + (v[6] + v[7]))

    for g, ref in enumerate((second, first)):
        for color in range(2):
            for t in range(2):
                tile = total(color, 2 * g + t)
                at = (2 * color + t) * 256
                ref[:, at: at + 128] = tile[:4]
                ref[:, at + 128: at + 256] = tile[4:]
    bucket[...] = jnp.sum(total(0, 4), axis=0, keepdims=True)


def last_sum(info, came):
    outs = (jax.ShapeDtypeStruct((4, 1024), F32), jax.ShapeDtypeStruct((4, 1024), F32), jax.ShapeDtypeStruct((1, 128), F32))
    return call(last_sum_kernel, outs, (info, came), 2, 2**16, 2**19)


def other_core(array):
    return lax.ppermute(array, "dp_2", [(0, 1), (1, 0)])


def step(clean, noise, t_index, bucket_id, bucket_count, w_first, w_second, teacher_first, teacher_second):
    total = clean.shape[0] * lax.axis_size(DP_OUTER)
    core, x, y = lax.axis_index("dp_2"), lax.axis_index("outer"), lax.axis_index("dp_0")
    info = jnp.stack([core, jnp.where(core == 0, x, y), jnp.where(core == 0, y, x)]).astype(jnp.int32)
    send_s, bucket, grad_out, pre_hi, inputs, act_hi = forward(
        info, t_index, bucket_id, bucket_count, clean, noise, w_first, w_second, teacher_first, teacher_second, total)
    came_s = other_core(send_s)
    keep_s = second_grad(info, act_hi, grad_out)
    send_f = first_grad(info, grad_out, pre_hi, inputs, w_second, True)
    came_f = other_core(send_f)
    second = around(info, *core_sum(info, keep_s, came_s, bucket))
    keep_f = first_grad(info, grad_out, pre_hi, inputs, w_second, False)
    first = around(info, *core_sum(info, keep_f, came_f))
    pieces = exchange(plane_sum(info, second, first), 1)
    came = lax.all_to_all(line_sum(info, pieces).reshape(16, 5, 8, 128), ("dp_1", "dp_2"), 0, 0, tiled=True)
    first_rows, second_rows, losses = last_sum(info, came)
    return first_rows, second_rows, losses[0, :BUCKETS]


def solution(mesh):
    split = Mesh(mesh.devices.reshape(4, 8, 2, mesh.shape["outer"]), DP_OUTER)
    placed = (P(DP_OUTER, None, None), P(DP_OUTER, None, None), P(DP_OUTER), P(DP_OUTER), P(), P(), P(), P(), P())
    return jax.shard_map(step, mesh=split, in_specs=placed,
                         out_specs=(P(DP_OUTER, None), P(DP_OUTER, None), P()), check_vma=False)
```

profile of v0, /device:TPU:7, one launch (start us, length us, event | category | flops | bytes accessed | tf_op | source)
XLA Modules:
  0.0 90.0 jit_solution(17264631073582982713)
XLA Ops:
  1.2 15.7 %forward.1 = (f32[513,8,128]{2,1,0:T(8,128)S(1)}, f32[8,128]{1,0:T(8,128)S(1)}, bf16[896,1024]{1,0:T(8,128)(2,1)S(1)}, f32[896,1024]{1,0:T(8,128)S(1)}, bf16[896...) custom-call(s32[3]{0:T(128)} %pad_add_fusion.place_hbm.info, s32[8]{0:T(128)} %t_index_hbm.1, s32[8]{0:T(128)} %bucket_id_hbm.1, ...), custom_call_target="tpu_custom_call" | custom-call | flops 8455716864 | bytes 25165824 | tf_op jit(solution)/shard_map/forward/pallas_call | solution.py:217
  17.0 0.9 %collective-permute-start = (f32[513,8,128]{2,1,0:T(8,128)S(1)}, f32[513,8,128]{2,1,0:T(8,128)S(1)}, u32[]{:S(2)}, u32[]{:S(2)}) collective-permute-start(f32[513,8,128]{2,1,0:T(8,128)S(1)} %get-tuple-element.32), channel_id=1, source_target_pairs={{0,4},{4,0},{1,5},{5,1},{2,6},{6,2},{3,7},{7,3},{8,12},{12,8},{9,1... | collective-permute-start | bytes 6303752 | tf_op jit(solution)/shard_map/ppermute | solution.py:397
  18.0 3.2 %first_grad.3 = f32[512,8,128]{2,1,0:T(8,128)S(1)} custom-call(s32[3]{0:T(128)S(1)} %copy-done.1, bf16[896,1024]{1,0:T(8,128)(2,1)S(1)} %get-tuple-element.31.grad_out, f32[896,1024]{1,0:T(8,128)S(1)} %get-tuple-element.41.pre_hi, bf16[896,1024]{1,0:T(8,128)(2,1)S(1)} %get-tuple-element.42.inputs, bf16[1024,1024]{1,0:T(8,128)(2,1)S(1)} %copy-done), custom_call_target="tpu_custom_call" | custom-call | flops 1879048192 | bytes 8388608 | tf_op jit(solution)/shard_map/first_grad/pallas_call | solution.py:247
  21.3 1.9 %second_grad.1.keep = f32[512,8,128]{2,1,0:T(8,128)S(1)} custom-call(s32[3]{0:T(128)S(1)} %copy-done.1, bf16[896,1024]{1,0:T(8,128)(2,1)S(1)} %get-tuple-element.30.act_hi, bf16[896,1024]{1,0:T(8,128)(2,1)S(1)} %get-tuple-element.31.grad_out), custom_call_target="tpu_custom_call" | custom-call | flops 939524096 | bytes 4194304 | tf_op jit(solution)/shard_map/second_grad/pallas_call | solution.py:235
  23.2 0.8 shard_map.112
  24.0 1.4 %collective-permute-start.1 = (f32[129,8,128]{2,1,0:T(8,128)S(1)}, f32[129,8,128]{2,1,0:T(8,128)S(1)}, u32[]{:S(2)}, u32[]{:S(2)}) collective-permute-start(f32[129,8,128]{2,1,0:T(8,128)S(1)} %get-tuple-element.35), channel_id=1, source_target_pairs={{0,1},{1,2},{2,3},{3,0},{4,68},{5,69},{6,70},{7,71},{8,9},{9,10},{... | collective-permute-start | bytes 1585160 | tf_op jit(solution)/shard_map/ppermute | solution.py:328
  25.4 1.5 %collective-permute-start.2 = (f32[129,8,128]{2,1,0:T(8,128)S(1)}, f32[129,8,128]{2,1,0:T(8,128)S(1)}, u32[]{:S(2)}, u32[]{:S(2)}) collective-permute-start(f32[129,8,128]{2,1,0:T(8,128)S(1)} %get-tuple-element.36), channel_id=1, source_target_pairs={{0,3},{1,0},{2,1},{3,2},{4,196},{5,197},{6,198},{7,199},{8,11},{9,... | collective-permute-start | bytes 1585160 | tf_op jit(solution)/shard_map/ppermute | solution.py:328
  26.9 3.2 %first_grad.2.keep = f32[512,8,128]{2,1,0:T(8,128)S(1)} custom-call(s32[3]{0:T(128)S(1)} %copy-done.1, bf16[896,1024]{1,0:T(8,128)(2,1)S(1)} %get-tuple-element.31.grad_out, f32[896,1024]{1,0:T(8,128)S(1)} %get-tuple-element.41.pre_hi, bf16[896,1024]{1,0:T(8,128)(2,1)S(1)} %get-tuple-element.42.inputs, bf16[1024,1024]{1,0:T(8,128)(2,1)S(1)} %copy-done), custom_call_target="tpu_custom_call" | custom-call | flops 1879048192 | bytes 8388608 | tf_op jit(solution)/shard_map/first_grad/pallas_call | solution.py:247
  30.2 0.8 shard_map.114
  31.0 2.7 %collective-permute-start.7 = (f32[128,8,128]{2,1,0:T(8,128)S(1)}, f32[128,8,128]{2,1,0:T(8,128)S(1)}, u32[]{:S(2)}, u32[]{:S(2)}) collective-permute-start(f32[128,8,128]{2,1,0:T(8,128)S(1)} %get-tuple-element.45), channel_id=1, source_target_pairs={{0,3},{1,0},{2,1},{3,2},{4,196},{5,197},{6,198},{7,199},{8,11},{9,... | collective-permute-start | bytes 1572872 | tf_op jit(solution)/shard_map/ppermute | solution.py:328
  34.4 1.4 %collective-permute-start.3 = (f32[65,8,128]{2,1,0:T(8,128)S(1)}, f32[65,8,128]{2,1,0:T(8,128)S(1)}, u32[]{:S(2)}, u32[]{:S(2)}) collective-permute-start(f32[65,8,128]{2,1,0:T(8,128)S(1)} %get-tuple-element.39), channel_id=1, source_target_pairs={{0,1},{1,2},{2,3},{3,0},{4,68},{5,69},{6,70},{7,71},{8,9},{9,10},{... | collective-permute-start | bytes 798728 | tf_op jit(solution)/shard_map/ppermute | solution.py:328
  35.7 4.8 %collective-permute-done.6.came_up.refs_6_ = f32[128,8,128]{2,1,0:T(8,128)S(1)} collective-permute-done((f32[128,8,128]{2,1,0:T(8,128)S(1)}, f32[128,8,128]{2,1,0:T(8,128)S(1)}, u32[]{:S(2)}, u32[]{:S(2)}) %collective-permute-start.6) | collective-permute-done | bytes 524320 | tf_op jit(solution)/shard_map/ppermute | solution.py:328
  41.3 2.6 %collective-permute-start.9 = (f32[64,8,128]{2,1,0:T(8,128)S(1)}, f32[64,8,128]{2,1,0:T(8,128)S(1)}, u32[]{:S(2)}, u32[]{:S(2)}) collective-permute-start(f32[64,8,128]{2,1,0:T(8,128)S(1)} %get-tuple-element.49), channel_id=1, source_target_pairs={{0,3},{1,0},{2,1},{3,2},{4,196},{5,197},{6,198},{7,199},{8,11},{9,... | collective-permute-start | bytes 786440 | tf_op jit(solution)/shard_map/ppermute | solution.py:328
  44.0 1.4 %collective-permute-start.4 = (f32[64,8,128]{2,1,0:T(8,128)S(1)}, f32[64,8,128]{2,1,0:T(8,128)S(1)}, u32[]{:S(2)}, u32[]{:S(2)}) collective-permute-start(f32[64,8,128]{2,1,0:T(8,128)S(1)} %get-tuple-element.40), channel_id=1, source_target_pairs={{0,3},{1,0},{2,1},{3,2},{4,196},{5,197},{6,198},{7,199},{8,11},{9,... | collective-permute-start | bytes 786440 | tf_op jit(solution)/shard_map/ppermute | solution.py:328
  45.4 2.3 %collective-permute-done.8.refs_8_ = f32[64,8,128]{2,1,0:T(8,128)S(1)} collective-permute-done((f32[64,8,128]{2,1,0:T(8,128)S(1)}, f32[64,8,128]{2,1,0:T(8,128)S(1)}, u32[]{:S(2)}, u32[]{:S(2)}) %collective-permute-start.8) | collective-permute-done | bytes 262176 | tf_op jit(solution)/shard_map/ppermute | solution.py:328
  47.7 2.5 %collective-permute-done.4.refs_4_ = f32[64,8,128]{2,1,0:T(8,128)S(1)} collective-permute-done((f32[64,8,128]{2,1,0:T(8,128)S(1)}, f32[64,8,128]{2,1,0:T(8,128)S(1)}, u32[]{:S(2)}, u32[]{:S(2)}) %collective-permute-start.4) | collective-permute-done | bytes 262176 | tf_op jit(solution)/shard_map/ppermute | solution.py:328
  50.1 0.8 shard_map.116
  50.9 1.8 %collective-permute-start.10 = (f32[65,8,128]{2,1,0:T(8,128)S(1)}, f32[65,8,128]{2,1,0:T(8,128)S(1)}, u32[]{:S(2)}, u32[]{:S(2)}) collective-permute-start(f32[65,8,128]{2,1,0:T(8,128)S(1)} %get-tuple-element.51), channel_id=1, source_target_pairs={{0,64},{1,65},{2,66},{3,67},{4,5},{5,6},{6,7},{7,4},{8,72},{9,73},... | collective-permute-start | bytes 798728 | tf_op jit(solution)/shard_map/ppermute | solution.py:328
  52.7 1.3 %collective-permute-start.12 = (f32[65,8,128]{2,1,0:T(8,128)S(1)}, f32[65,8,128]{2,1,0:T(8,128)S(1)}, u32[]{:S(2)}, u32[]{:S(2)}) collective-permute-start(f32[65,8,128]{2,1,0:T(8,128)S(1)} %get-tuple-element.53), channel_id=1, source_target_pairs={{0,128},{1,129},{2,130},{3,131},{4,6},{5,7},{6,4},{7,5},{8,136},{9... | collective-permute-start | bytes 798728 | tf_op jit(solution)/shard_map/ppermute | solution.py:328
  54.0 2.2 %collective-permute-done.10.b = f32[65,8,128]{2,1,0:T(8,128)S(1)} collective-permute-done((f32[65,8,128]{2,1,0:T(8,128)S(1)}, f32[65,8,128]{2,1,0:T(8,128)S(1)}, u32[]{:S(2)}, u32[]{:S(2)}) %collective-permute-start.10) | collective-permute-done | bytes 266272 | tf_op jit(solution)/shard_map/ppermute | solution.py:328
  56.2 6.1 %collective-permute-done.11.c = f32[65,8,128]{2,1,0:T(8,128)S(1)} collective-permute-done((f32[65,8,128]{2,1,0:T(8,128)S(1)}, f32[65,8,128]{2,1,0:T(8,128)S(1)}, u32[]{:S(2)}, u32[]{:S(2)}) %collective-permute-start.11) | collective-permute-done | bytes 266272 | tf_op jit(solution)/shard_map/ppermute | solution.py:328
  62.3 0.6 shard_map.117
  63.0 25.4 %all_to_all.5.came = f32[16,5,8,128]{3,2,1,0:T(8,128)S(1)} all-to-all(f32[16,5,8,128]{3,2,1,0:T(8,128)S(1)} %bitcast.6), channel_id=1, replica_groups=mesh['dp_0'=4,'dp_1'=8,'dp_2'=2,'outer'=4] {'dp_1','dp_2'}, dimensions={0} | all-to-all | bytes 655360 | tf_op jit(solution)/shard_map/all_to_all | solution.py:414
  88.3 1.2 %shard_map.118 = (f32[4,1024]{1,0:T(4,128)}, f32[4,1024]{1,0:T(4,128)}, f32[1,128]{1,0:T(1,128)S(1)}) custom-call(s32[3]{0:T(128)S(1)} %copy-done.1, f32[16,5,8,128]{3,2,1,0:T(8,128)S(1)} %all_to_all.5.came), custom_call_target="tpu_custom_call" | custom-call | flops 65536 | bytes 524288 | tf_op jit(solution)/shard_map/pallas_call | solution.py:260
  (20 shorter events, 2.8 us)
Async XLA Ops:
  1.2 16.7 %copy-start = (bf16[1024,1024]{1,0:T(8,128)(2,1)S(1)}, bf16[1024,1024]{1,0:T(8,128)(2,1)}, u32[]{:S(2)}) copy-start(bf16[1024,1024]{1,0:T(8,128)(2,1)} %w2.5) | copy-start | bytes 6291460
  1.2 16.7 %copy-start.1 = (s32[3]{0:T(128)S(1)}, s32[3]{0:T(128)}, u32[]{:S(2)}) copy-start(s32[3]{0:T(128)} %pad_add_fusion.place_hbm.info) | copy-start | bytes 40
  17.0 6.2 %collective-permute-start = (f32[513,8,128]{2,1,0:T(8,128)S(1)}, f32[513,8,128]{2,1,0:T(8,128)S(1)}, u32[]{:S(2)}, u32[]{:S(2)}) collective-permute-start(f32[513,8,128]{2,1,0:T(8,128)S(1)} %get-tuple-element.32), channel_id=1, source_target_pairs={{0,4},{4,0},{1,5},{5,1},{2,6},{6,2},{3,7},{7,3},{8,12},{12,8},{9,1... | collective-permute-start | bytes 6303752 | tf_op jit(solution)/shard_map/ppermute | solution.py:397
  21.2 9.0 %collective-permute-start.5 = (f32[512,8,128]{2,1,0:T(8,128)S(1)}, f32[512,8,128]{2,1,0:T(8,128)S(1)}, u32[]{:S(2)}, u32[]{:S(2)}) collective-permute-start(f32[512,8,128]{2,1,0:T(8,128)S(1)} %first_grad.3), channel_id=1, source_target_pairs={{0,4},{4,0},{1,5},{5,1},{2,6},{6,2},{3,7},{7,3},{8,12},{12,8},{9,1... | collective-permute-start | bytes 6291464 | tf_op jit(solution)/shard_map/ppermute | solution.py:397
  24.0 9.7 %collective-permute-start.1 = (f32[129,8,128]{2,1,0:T(8,128)S(1)}, f32[129,8,128]{2,1,0:T(8,128)S(1)}, u32[]{:S(2)}, u32[]{:S(2)}) collective-permute-start(f32[129,8,128]{2,1,0:T(8,128)S(1)} %get-tuple-element.35), channel_id=1, source_target_pairs={{0,1},{1,2},{2,3},{3,0},{4,68},{5,69},{6,70},{7,71},{8,9},{9,10},{... | collective-permute-start | bytes 1585160 | tf_op jit(solution)/shard_map/ppermute | solution.py:328
  25.4 8.4 %collective-permute-start.2 = (f32[129,8,128]{2,1,0:T(8,128)S(1)}, f32[129,8,128]{2,1,0:T(8,128)S(1)}, u32[]{:S(2)}, u32[]{:S(2)}) collective-permute-start(f32[129,8,128]{2,1,0:T(8,128)S(1)} %get-tuple-element.36), channel_id=1, source_target_pairs={{0,3},{1,0},{2,1},{3,2},{4,196},{5,197},{6,198},{7,199},{8,11},{9,... | collective-permute-start | bytes 1585160 | tf_op jit(solution)/shard_map/ppermute | solution.py:328
  30.9 9.6 %collective-permute-start.6 = (f32[128,8,128]{2,1,0:T(8,128)S(1)}, f32[128,8,128]{2,1,0:T(8,128)S(1)}, u32[]{:S(2)}, u32[]{:S(2)}) collective-permute-start(f32[128,8,128]{2,1,0:T(8,128)S(1)} %get-tuple-element.44), channel_id=1, source_target_pairs={{0,1},{1,2},{2,3},{3,0},{4,68},{5,69},{6,70},{7,71},{8,9},{9,10},{... | collective-permute-start | bytes 1572872 | tf_op jit(solution)/shard_map/ppermute | solution.py:328
  31.0 9.5 %collective-permute-start.7 = (f32[128,8,128]{2,1,0:T(8,128)S(1)}, f32[128,8,128]{2,1,0:T(8,128)S(1)}, u32[]{:S(2)}, u32[]{:S(2)}) collective-permute-start(f32[128,8,128]{2,1,0:T(8,128)S(1)} %get-tuple-element.45), channel_id=1, source_target_pairs={{0,3},{1,0},{2,1},{3,2},{4,196},{5,197},{6,198},{7,199},{8,11},{9,... | collective-permute-start | bytes 1572872 | tf_op jit(solution)/shard_map/ppermute | solution.py:328
  34.4 15.8 %collective-permute-start.3 = (f32[65,8,128]{2,1,0:T(8,128)S(1)}, f32[65,8,128]{2,1,0:T(8,128)S(1)}, u32[]{:S(2)}, u32[]{:S(2)}) collective-permute-start(f32[65,8,128]{2,1,0:T(8,128)S(1)} %get-tuple-element.39), channel_id=1, source_target_pairs={{0,1},{1,2},{2,3},{3,0},{4,68},{5,69},{6,70},{7,71},{8,9},{9,10},{... | collective-permute-start | bytes 798728 | tf_op jit(solution)/shard_map/ppermute | solution.py:328
  41.2 6.5 %collective-permute-start.8 = (f32[64,8,128]{2,1,0:T(8,128)S(1)}, f32[64,8,128]{2,1,0:T(8,128)S(1)}, u32[]{:S(2)}, u32[]{:S(2)}) collective-permute-start(f32[64,8,128]{2,1,0:T(8,128)S(1)} %get-tuple-element.48), channel_id=1, source_target_pairs={{0,1},{1,2},{2,3},{3,0},{4,68},{5,69},{6,70},{7,71},{8,9},{9,10},{... | collective-permute-start | bytes 786440 | tf_op jit(solution)/shard_map/ppermute | solution.py:328
  41.3 6.3 %collective-permute-start.9 = (f32[64,8,128]{2,1,0:T(8,128)S(1)}, f32[64,8,128]{2,1,0:T(8,128)S(1)}, u32[]{:S(2)}, u32[]{:S(2)}) collective-permute-start(f32[64,8,128]{2,1,0:T(8,128)S(1)} %get-tuple-element.49), channel_id=1, source_target_pairs={{0,3},{1,0},{2,1},{3,2},{4,196},{5,197},{6,198},{7,199},{8,11},{9,... | collective-permute-start | bytes 786440 | tf_op jit(solution)/shard_map/ppermute | solution.py:328
  44.0 6.1 %collective-permute-start.4 = (f32[64,8,128]{2,1,0:T(8,128)S(1)}, f32[64,8,128]{2,1,0:T(8,128)S(1)}, u32[]{:S(2)}, u32[]{:S(2)}) collective-permute-start(f32[64,8,128]{2,1,0:T(8,128)S(1)} %get-tuple-element.40), channel_id=1, source_target_pairs={{0,3},{1,0},{2,1},{3,2},{4,196},{5,197},{6,198},{7,199},{8,11},{9,... | collective-permute-start | bytes 786440 | tf_op jit(solution)/shard_map/ppermute | solution.py:328
  50.9 5.3 %collective-permute-start.10 = (f32[65,8,128]{2,1,0:T(8,128)S(1)}, f32[65,8,128]{2,1,0:T(8,128)S(1)}, u32[]{:S(2)}, u32[]{:S(2)}) collective-permute-start(f32[65,8,128]{2,1,0:T(8,128)S(1)} %get-tuple-element.51), channel_id=1, source_target_pairs={{0,64},{1,65},{2,66},{3,67},{4,5},{5,6},{6,7},{7,4},{8,72},{9,73},... | collective-permute-start | bytes 798728 | tf_op jit(solution)/shard_map/ppermute | solution.py:328
  52.7 9.6 %collective-permute-start.11 = (f32[65,8,128]{2,1,0:T(8,128)S(1)}, f32[65,8,128]{2,1,0:T(8,128)S(1)}, u32[]{:S(2)}, u32[]{:S(2)}) collective-permute-start(f32[65,8,128]{2,1,0:T(8,128)S(1)} %get-tuple-element.52), channel_id=1, source_target_pairs={{0,192},{1,193},{2,194},{3,195},{4,7},{5,4},{6,5},{7,6},{8,200},{9... | collective-permute-start | bytes 798728 | tf_op jit(solution)/shard_map/ppermute | solution.py:328
  52.7 9.6 %collective-permute-start.12 = (f32[65,8,128]{2,1,0:T(8,128)S(1)}, f32[65,8,128]{2,1,0:T(8,128)S(1)}, u32[]{:S(2)}, u32[]{:S(2)}) collective-permute-start(f32[65,8,128]{2,1,0:T(8,128)S(1)} %get-tuple-element.53), channel_id=1, source_target_pairs={{0,128},{1,129},{2,130},{3,131},{4,6},{5,7},{6,4},{7,5},{8,136},{9... | collective-permute-start | bytes 798728 | tf_op jit(solution)/shard_map/ppermute | solution.py:328
where the time goes:
time: 90.1 us; the launch traced here: 90 us
  Pallas kernels  29.4 us (33%)
  blocking collectives  25.4 us (28%)
  waiting for transfers between devices  18 us (20%)
  starting transfers between devices  15.4 us (17%)
    all_to_all x1, blocking collectives, step(): lax.all_to_all(line_sum(info, pieces).reshape(16, 5, 8, 128), ('dp_1', 'd...  25.4 us
    ppermute x11, waiting for transfers between devices, shift(): return lax.ppermute(piece, DP_OUTER, shift_pairs(k, x_on_core))  18 us
    pallas_call x1, Pallas kernels, forward(): pl.pallas_call(functools.partial(forward_kernel, total=total), out_shape=...  15.7 us
    ppermute x11, starting transfers between devices, shift(): return lax.ppermute(piece, DP_OUTER, shift_pairs(k, x_on_core))  14.3 us
    pallas_call x2, Pallas kernels, first_grad(): pl.pallas_call(functools.partial(first_kernel, color_flip=color_flip), ou...  6.47 us
    pallas_call x7, Pallas kernels, call(): pl.pallas_call(kernel, out_shape=outs, in_specs=[SMEM] + [VMEM] * (len(in...  5.28 us
    pallas_call x1, Pallas kernels, second_grad(): pl.pallas_call(second_kernel, out_shape=pltpu.VMEM((512, 8, 128), F32), i...  1.9 us
  transfers between devices with their start and end apart: 13, of which 5 were waited for; matrix products, arithmetic and copies ran while one was open for 0% of the time, Pallas kernels for 12%

commit v1 on v0

--- a/solution.py
+++ b/solution.py
@@ -20,10 +20,17 @@
 TILE = (8, 128)
 TN = 256
 MB = 448
-CORE, FIRST_AT, SECOND_AT = 0, 1, 2
 VMEM = pl.BlockSpec(memory_space=pltpu.VMEM)
-SMEM = pl.BlockSpec(memory_space=pltpu.SMEM)
 ANY = pl.BlockSpec(memory_space=pltpu.HBM)
+
+
+def core_index():
+    return lax.axis_index("dp_2")
+
+
+def along(first, ahead):
+    on_x = core_index() == (0 if first else 1)
+    return (jnp.where(on_x, lax.axis_index("outer"), lax.axis_index("dp_0")) + ahead) % 4
 
 
 def rows_from(values):
@@ -86,12 +93,12 @@
     return pl.ds(pl.multiple_of(color * 512, 512), 512)
 
 
-def forward_kernel(place_hbm, t_index_hbm, bucket_id_hbm, bucket_count_hbm, clean_hbm, noise_hbm, w1, w2, t1, t2,
+def forward_kernel(t_index_hbm, bucket_id_hbm, bucket_count_hbm, clean_hbm, noise_hbm, w1, w2, t1, t2,
                    send, bucket, grad_out, pre_hi, inputs, act_hi,
-                   clean, noise, in_lo, act_lo, diff, coef, wbuf, place, t_index, bucket_id, bucket_count,
+                   clean, noise, in_lo, act_lo, diff, coef, wbuf, t_index, bucket_id, bucket_count,
                    field_sems, sems, small_sems, *, total):
     small = [pltpu.make_async_copy(src, dst, small_sems.at[k]) for k, (src, dst) in enumerate((
-        (place_hbm, place), (t_index_hbm, t_index), (bucket_id_hbm, bucket_id), (bucket_count_hbm, bucket_count)))]
+        (t_index_hbm, t_index), (bucket_id_hbm, bucket_id), (bucket_count_hbm, bucket_count)))]
     fields = []
     for lat in range(LAT):
         rows = pl.ds(lat * PATCHES, PATCHES)
@@ -182,16 +189,16 @@
     for lat in range(LAT):
         rows = block_rows(lat)
         grad_out[rows, :] = (one(8, lat) * diff[rows, :]).astype(BF16)
-    color = 1 - place[CORE]
+    color = 1 - core_index()
     weight_gradient(act_hi, grad_out, half(color), color, send)
 
 
-def second_kernel(info, act_hi, grad_out, keep):
-    weight_gradient(act_hi, grad_out, half(info[CORE]), info[CORE], keep)
-
-
-def first_kernel(info, grad_out, pre_hi, inputs, w2, out, grad_pre, *, color_flip):
-    color = 1 - info[CORE] if color_flip else info[CORE]
+def second_kernel(act_hi, grad_out, keep):
+    weight_gradient(act_hi, grad_out, half(core_index()), core_index(), keep)
+
+
+def first_kernel(grad_out, pre_hi, inputs, w2, out, grad_pre, *, color_flip):
+    color = 1 - core_index() if color_flip else core_index()
     cols = half(color)
 
     def back(m, _):
@@ -213,65 +220,65 @@
 PRODUCT = 2 * ROWS * D * H
 
 
-def forward(info, t_index, bucket_id, bucket_count, clean, noise, w1, w2, t1, t2, total):
+def forward(t_index, bucket_id, bucket_count, clean, noise, w1, w2, t1, t2, total):
     return pl.pallas_call(
         functools.partial(forward_kernel, total=total),
         out_shape=(pltpu.VMEM((513, 8, 128), F32), pltpu.VMEM(TILE, F32), pltpu.VMEM((ROWS, D), BF16),
                    pltpu.VMEM((ROWS, H), F32), pltpu.VMEM((ROWS, D), BF16), pltpu.VMEM((ROWS, H), BF16)),
-        in_specs=[ANY] * 10,
+        in_specs=[ANY] * 9,
         out_specs=(VMEM,) * 6,
         scratch_shapes=[pltpu.VMEM((ROWS, D), BF16), pltpu.VMEM((ROWS, D), BF16), pltpu.VMEM((ROWS, D), BF16),
                         pltpu.VMEM((ROWS, H), BF16), pltpu.VMEM((ROWS, D), F32), pltpu.VMEM((9,) + TILE, F32),
-                        pltpu.VMEM((4, D, H), BF16), pltpu.SMEM((3,), jnp.int32), pltpu.SMEM((LAT,), jnp.int32),
+                        pltpu.VMEM((4, D, H), BF16), pltpu.SMEM((LAT,), jnp.int32),
                         pltpu.SMEM((LAT,), jnp.int32), pltpu.SMEM((BUCKETS,), jnp.int32),
-                        pltpu.SemaphoreType.DMA((2, LAT)), pltpu.SemaphoreType.DMA((4,)), pltpu.SemaphoreType.DMA((4,))],
+                        pltpu.SemaphoreType.DMA((2, LAT)), pltpu.SemaphoreType.DMA((4,)), pltpu.SemaphoreType.DMA((3,))],
         compiler_params=pltpu.CompilerParams(vmem_limit_bytes=51 * 2**20),
         cost_estimate=pl.CostEstimate(flops=9 * PRODUCT // 2, bytes_accessed=24 * 2**20, transcendentals=2 * ROWS * H),
         name="forward",
-    )(info, t_index, bucket_id, bucket_count, clean, noise, w1, w2, t1, t2)
-
-
-def second_grad(info, act_hi, grad_out):
+    )(t_index, bucket_id, bucket_count, clean, noise, w1, w2, t1, t2)
+
+
+def second_grad(act_hi, grad_out):
     return pl.pallas_call(
         second_kernel,
         out_shape=pltpu.VMEM((512, 8, 128), F32),
-        in_specs=[SMEM, VMEM, VMEM],
+        in_specs=[VMEM, VMEM],
         out_specs=VMEM,
         compiler_params=pltpu.CompilerParams(vmem_limit_bytes=16 * 2**20),
         cost_estimate=pl.CostEstimate(flops=PRODUCT // 2, bytes_accessed=4 * 2**20, transcendentals=0),
         name="second_grad",
-    )(info, act_hi, grad_out)
-
-
-def first_grad(info, grad_out, pre_hi, inputs, w2, color_flip, rows=pltpu.VMEM((512, 8, 128), F32)):
+    )(act_hi, grad_out)
+
+
+def first_grad(grad_out, pre_hi, inputs, w2, color_flip, rows=pltpu.VMEM((512, 8, 128), F32)):
     return pl.pallas_call(
         functools.partial(first_kernel, color_flip=color_flip),
         out_shape=rows,
-        in_specs=[SMEM] + [VMEM] * 4,
+        in_specs=[VMEM] * 4,
         out_specs=VMEM,
         scratch_shapes=[pltpu.VMEM((ROWS, 512), BF16)],
         compiler_params=pltpu.CompilerParams(vmem_limit_bytes=20 * 2**20),
         cost_estimate=pl.CostEstimate(flops=PRODUCT, bytes_accessed=8 * 2**20, transcendentals=0),
         name="first_grad",
-    )(info, grad_out, pre_hi, inputs, w2)
+    )(grad_out, pre_hi, inputs, w2)
 
 
 def call(kernel, outs, ins, vmem_mib, flops, moved):
     return pl.pallas_call(
         kernel,
         out_shape=outs,
-        in_specs=[SMEM] + [VMEM] * (len(ins) - 1),
+        in_specs=[VMEM] * len(ins),
         out_specs=tuple(VMEM for _ in outs),
         compiler_params=pltpu.CompilerParams(vmem_limit_bytes=vmem_mib * 2**20),
         cost_estimate=pl.CostEstimate(flops=flops, bytes_accessed=moved, transcendentals=0),
     )(*ins)
 
 
-def core_sum_kernel(info, keep, came, *rest, with_bucket):
+def core_sum_kernel(keep, came, *rest, with_bucket):
     bucket, (own, up, down, up_kept, down_kept) = (rest[0], rest[1:]) if with_bucket else (None, rest)
 
     def half(ref, at, ahead, t):
-        p = (info[FIRST_AT] + ahead) % 4
+        p = along(True, ahead)
         for q in range(4):
             src = pl.ds(pl.multiple_of(p * 128, 128) + q * 32 + t * 16, 16)
             ref[pl.ds(at + q * 16, 16)] = keep[src] + came[src]
@@ -282,7 +289,7 @@
     half(down, 64, 3, 0)
     half(up_kept, 0, 1, 0)
     half(down_kept, 0, 3, 1)
-    src = pl.ds(pl.multiple_of(info[FIRST_AT] * 128, 128), 128)
+    src = pl.ds(pl.multiple_of(along(True, 0) * 128, 128), 128)
     own[pl.ds(0, 128)] = keep[src] + came[src]
     if with_bucket:
         both = bucket[...] + came[512]
@@ -292,25 +299,22 @@
         up_kept[64] = both
 
 
-def core_sum(info, keep, came, bucket=None):
+def core_sum(keep, came, bucket=None):
     more = 0 if bucket is None else 1
     outs = (tiles(128 + more),) * 3 + (tiles(64 + more), tiles(64))
-    ins = (info, keep, came) if bucket is None else (info, keep, came, bucket)
+    ins = (keep, came) if bucket is None else (keep, came, bucket)
     return call(functools.partial(core_sum_kernel, with_bucket=bucket is not None), outs, ins,
                 10, 2**19, 6 * 2**20)
 
 
-def middle_sum_kernel(info, came_up, came_down, up_kept, down_kept, up, down):
-    up[pl.ds(0, 64)] = up_kept[pl.ds(0, 64)] + came_up[pl.ds(0, 64)]
-    down[...] = down_kept[...] + came_down[pl.ds(0, 64)]
-    if up.shape[0] > 64:
-        up[64] = up_kept[64] + came_up[128]
-
-
-def middle_sum(info, came_up, came_down, up_kept, down_kept):
-    outs = (tiles(up_kept.shape[0]), tiles(64))
-    return call(middle_sum_kernel, outs, (info, came_up, came_down, up_kept, down_kept),
-                4, 2**17, 3 * 2**19)
+def middle_sum_kernel(came, kept, out):
+    out[pl.ds(0, 64)] = kept[pl.ds(0, 64)] + came[pl.ds(0, 64)]
+    if out.shape[0] > 64:
+        out[64] = kept[64] + came[128]
+
+
+def middle_sum(came, kept):
+    return call(middle_sum_kernel, (tiles(kept.shape[0]),), (came, kept), 3, 2**16, 3 * 2**18)[0]
 
 
 def shift_pairs(k, x_on_core):
@@ -328,18 +332,19 @@
     return lax.ppermute(piece, DP_OUTER, shift_pairs(k, x_on_core))
 
 
-def around(info, own, up, down, up_kept, down_kept):
+def around(own, up, down, up_kept, down_kept):
     came_up, came_down = shift(up, 1, 0), shift(down, 3, 0)
-    up, down = middle_sum(info, came_up, came_down, up_kept, down_kept)
+    up = middle_sum(came_up, up_kept)
     up = shift(up, 1, 0)
+    down = middle_sum(came_down, down_kept)
     down = shift(down, 3, 0)
     return own, came_up, came_down, up, down
 
 
-def plane_sum_kernel(info, *refs):
+def plane_sum_kernel(*refs):
     second, first, pieces = refs[:5], refs[5:10], refs[10:]
     for k in range(4):
-        q = (info[SECOND_AT] + k) % 4
+        q = along(False, k)
         for g, (own, came_up, came_down, up, down) in enumerate((second, first)):
             here = pl.multiple_of(q * 32, 32)
             there = pl.multiple_of(q * 16, 16)
@@ -348,15 +353,15 @@
         pieces[k][64] = second[0][128] + second[3][64] + second[2][128]
 
 
-def plane_sum(info, second, first):
-    return call(plane_sum_kernel, (tiles(65),) * 4, (info, *second, *first), 10, 2**20, 5 * 2**20)
+def plane_sum(second, first):
+    return call(plane_sum_kernel, (tiles(65),) * 4, (*second, *first), 10, 2**20, 5 * 2**20)
 
 
 def exchange(pieces, x_on_core):
     return [pieces[0]] + [shift(pieces[k], k, x_on_core) for k in (1, 3, 2)]
 
 
-def line_sum_kernel(info, a, b, c, d, out):
+def line_sum_kernel(a, b, c, d, out):
     for g in range(2):
         for t in range(2):
             for core in range(2):
@@ -368,12 +373,12 @@
             out[z, core, 4] = bucket
 
 
-def line_sum(info, pieces):
+def line_sum(pieces):
     outs = (jax.ShapeDtypeStruct((8, 2, 5, 8, 128), F32),)
-    return call(line_sum_kernel, outs, (info, *pieces), 4, 2**18, 2**20)[0]
-
-
-def last_sum_kernel(info, came, first, second, bucket):
+    return call(line_sum_kernel, outs, tuple(pieces), 4, 2**18, 2**20)[0]
+
+
+def last_sum_kernel(came, first, second, bucket):
     def total(color, at):
         v = [came[2 * z + color, at] for z in range(8)]
         return ((v[0] + v[1]) + (v[2] + v[3])) + ((v[4] + v[5]) + (v[6] + v[7]))
@@ -385,12 +390,12 @@
                 at = (2 * color + t) * 256
                 ref[:, at: at + 128] = tile[:4]
                 ref[:, at + 128: at + 256] = tile[4:]
-    bucket[...] = jnp.sum(total(0, 4), axis=0, keepdims=True)
-
-
-def last_sum(info, came):
-    outs = (jax.ShapeDtypeStruct((4, 1024), F32), jax.ShapeDtypeStruct((4, 1024), F32), jax.ShapeDtypeStruct((1, 128), F32))
-    return call(last_sum_kernel, outs, (info, came), 2, 2**16, 2**19)
+    bucket[...] = jnp.sum(total(0, 4), axis=0, keepdims=True)[:, :BUCKETS]
+
+
+def last_sum(came):
+    outs = (jax.ShapeDtypeStruct((4, 1024), F32), jax.ShapeDtypeStruct((4, 1024), F32), jax.ShapeDtypeStruct((1, BUCKETS), F32))
+    return call(last_sum_kernel, outs, (came,), 2, 2**16, 2**19)
 
 
 def other_core(array):
@@ -399,21 +404,19 @@
 
 def step(clean, noise, t_index, bucket_id, bucket_count, w_first, w_second, teacher_first, teacher_second):
     total = clean.shape[0] * lax.axis_size(DP_OUTER)
-    core, x, y = lax.axis_index("dp_2"), lax.axis_index("outer"), lax.axis_index("dp_0")
-    info = jnp.stack([core, jnp.where(core == 0, x, y), jnp.where(core == 0, y, x)]).astype(jnp.int32)
     send_s, bucket, grad_out, pre_hi, inputs, act_hi = forward(
-        info, t_index, bucket_id, bucket_count, clean, noise, w_first, w_second, teacher_first, teacher_second, total)
+        t_index, bucket_id, bucket_count, clean, noise, w_first, w_second, teacher_first, teacher_second, total)
     came_s = other_core(send_s)
-    keep_s = second_grad(info, act_hi, grad_out)
-    send_f = first_grad(info, grad_out, pre_hi, inputs, w_second, True)
+    keep_s = second_grad(act_hi, grad_out)
+    send_f = first_grad(grad_out, pre_hi, inputs, w_second, True)
     came_f = other_core(send_f)
-    second = around(info, *core_sum(info, keep_s, came_s, bucket))
-    keep_f = first_grad(info, grad_out, pre_hi, inputs, w_second, False)
-    first = around(info, *core_sum(info, keep_f, came_f))
-    pieces = exchange(plane_sum(info, second, first), 1)
-    came = lax.all_to_all(line_sum(info, pieces).reshape(16, 5, 8, 128), ("dp_1", "dp_2"), 0, 0, tiled=True)
-    first_rows, second_rows, losses = last_sum(info, came)
-    return first_rows, second_rows, losses[0, :BUCKETS]
+    second = around(*core_sum(keep_s, came_s, bucket))
+    keep_f = first_grad(grad_out, pre_hi, inputs, w_second, False)
+    first = around(*core_sum(keep_f, came_f))
+    pieces = exchange(plane_sum(second, first), 1)
+    came = lax.all_to_all(line_sum(pieces).reshape(16, 5, 8, 128), ("dp_1", "dp_2"), 0, 0, tiled=True)
+    first_rows, second_rows, losses = last_sum(came)
+    return first_rows, second_rows, losses.reshape(BUCKETS)
 
 
 def solution(mesh):

time: 90.1 us -> 84.1 us (0.933)
  Pallas kernels: 29.4 us -> 24 us
  waiting for transfers between devices: 18 us -> 20.7 us
  starting transfers between devices: 15.4 us -> 13.2 us
    pallas_call x7 -> x9, Pallas kernels: 5.28 us -> 1.51 us  [call(): pl.pallas_call(kernel, out_shape=outs, in_specs=[VMEM] * len(ins), out_sp...]
    ppermute x11, waiting for transfers between devices: 18 us -> 20.7 us  [shift(): return lax.ppermute(piece, DP_OUTER, shift_pairs(k, x_on_core))]
    ppermute x11, starting transfers between devices: 14.3 us -> 12.1 us  [shift(): return lax.ppermute(piece, DP_OUTER, shift_pairs(k, x_on_core))]
    pallas_call x2, Pallas kernels: 6.47 us -> 5.38 us  [first_grad(): pl.pallas_call(functools.partial(first_kernel, color_flip=color_flip), ou...]
  transfers between devices with their start and end apart: 13 -> 13, of which waited for: 5 -> 6; matrix products, arithmetic and copies ran while one was open for 0% -> 0% of each run, Pallas kernels for 12% -> 9%
where the time goes in v1:
time: 84.1 us; the launch traced here: 84 us
  blocking collectives  25.4 us (30%)
  Pallas kernels  24 us (29%)
  waiting for transfers between devices  20.7 us (25%)
  starting transfers between devices  13.2 us (16%)
    all_to_all x1, blocking collectives, step(): lax.all_to_all(line_sum(pieces).reshape(16, 5, 8, 128), ('dp_1', 'dp_2'),...  25.4 us
    ppermute x11, waiting for transfers between devices, shift(): return lax.ppermute(piece, DP_OUTER, shift_pairs(k, x_on_core))  20.7 us
    pallas_call x1, Pallas kernels, forward(): pl.pallas_call(functools.partial(forward_kernel, total=total), out_shape=...  15.7 us
    ppermute x11, starting transfers between devices, shift(): return lax.ppermute(piece, DP_OUTER, shift_pairs(k, x_on_core))  12.1 us
    pallas_call x2, Pallas kernels, first_grad(): pl.pallas_call(functools.partial(first_kernel, color_flip=color_flip), ou...  5.38 us
  transfers between devices with their start and end apart: 13, of which 6 were waited for; matrix products, arithmetic and copies ran while one was open for 0% of the time, Pallas kernels for 9%

profile of v1, /device:TPU:7, one launch (start us, length us, event | category | flops | bytes accessed | tf_op | source)
XLA Modules:
  0.0 84.0 jit_solution(5190488733099866958)
XLA Ops:
  0.6 15.7 %forward.1 = (f32[513,8,128]{2,1,0:T(8,128)S(1)}, f32[8,128]{1,0:T(8,128)S(1)}, bf16[896,1024]{1,0:T(8,128)(2,1)S(1)}, f32[896,1024]{1,0:T(8,128)S(1)}, bf16[896...) custom-call(s32[8]{0:T(128)} %t_index_hbm.1, s32[8]{0:T(128)} %bucket_id_hbm.1, s32[16]{0:T(128)} %bucket_count_hbm.1, ...), custom_call_target="tpu_custom_call" | custom-call | flops 8455716864 | bytes 25165824 | tf_op jit(solution)/shard_map/forward/pallas_call | solution.py:224
  16.4 1.0 %collective-permute-start = (f32[513,8,128]{2,1,0:T(8,128)S(1)}, f32[513,8,128]{2,1,0:T(8,128)S(1)}, u32[]{:S(2)}, u32[]{:S(2)}) collective-permute-start(f32[513,8,128]{2,1,0:T(8,128)S(1)} %get-tuple-element.28), channel_id=1, source_target_pairs={{0,4},{4,0},{1,5},{5,1},{2,6},{6,2},{3,7},{7,3},{8,12},{12,8},{9,1... | collective-permute-start | bytes 6303752 | tf_op jit(solution)/shard_map/ppermute | solution.py:402
  17.3 2.7 %first_grad.3 = f32[512,8,128]{2,1,0:T(8,128)S(1)} custom-call(bf16[896,1024]{1,0:T(8,128)(2,1)S(1)} %get-tuple-element.27.grad_out, f32[896,1024]{1,0:T(8,128)S(1)} %get-tuple-element.35.pre_hi, bf16[896,1024]{1,0:T(8,128)(2,1)S(1)} %get-tuple-element.36.inputs, bf16[1024,1024]{1,0:T(8,128)(2,1)S(1)} %copy-done), custom_call_target="tpu_custom_call" | custom-call | flops 1879048192 | bytes 8388608 | tf_op jit(solution)/shard_map/first_grad/pallas_call | solution.py:254
  20.1 1.4 %second_grad.1.keep = f32[512,8,128]{2,1,0:T(8,128)S(1)} custom-call(bf16[896,1024]{1,0:T(8,128)(2,1)S(1)} %get-tuple-element.26.act_hi, bf16[896,1024]{1,0:T(8,128)(2,1)S(1)} %get-tuple-element.27.grad_out), custom_call_target="tpu_custom_call" | custom-call | flops 939524096 | bytes 4194304 | tf_op jit(solution)/shard_map/second_grad/pallas_call | solution.py:242
  21.5 0.2 shard_map.112
  21.8 1.4 %collective-permute-start.1 = (f32[129,8,128]{2,1,0:T(8,128)S(1)}, f32[129,8,128]{2,1,0:T(8,128)S(1)}, u32[]{:S(2)}, u32[]{:S(2)}) collective-permute-start(f32[129,8,128]{2,1,0:T(8,128)S(1)} %get-tuple-element.31), channel_id=1, source_target_pairs={{0,1},{1,2},{2,3},{3,0},{4,68},{5,69},{6,70},{7,71},{8,9},{9,10},{... | collective-permute-start | bytes 1585160 | tf_op jit(solution)/shard_map/ppermute | solution.py:332
  23.2 1.5 %collective-permute-start.2 = (f32[129,8,128]{2,1,0:T(8,128)S(1)}, f32[129,8,128]{2,1,0:T(8,128)S(1)}, u32[]{:S(2)}, u32[]{:S(2)}) collective-permute-start(f32[129,8,128]{2,1,0:T(8,128)S(1)} %get-tuple-element.32), channel_id=1, source_target_pairs={{0,3},{1,0},{2,1},{3,2},{4,196},{5,197},{6,198},{7,199},{8,11},{9,... | collective-permute-start | bytes 1585160 | tf_op jit(solution)/shard_map/ppermute | solution.py:332
  24.7 2.7 %first_grad.2.keep = f32[512,8,128]{2,1,0:T(8,128)S(1)} custom-call(bf16[896,1024]{1,0:T(8,128)(2,1)S(1)} %get-tuple-element.27.grad_out, f32[896,1024]{1,0:T(8,128)S(1)} %get-tuple-element.35.pre_hi, bf16[896,1024]{1,0:T(8,128)(2,1)S(1)} %get-tuple-element.36.inputs, bf16[1024,1024]{1,0:T(8,128)(2,1)S(1)} %copy-done), custom_call_target="tpu_custom_call" | custom-call | flops 1879048192 | bytes 8388608 | tf_op jit(solution)/shard_map/first_grad/pallas_call | solution.py:254
  27.4 0.2 shard_map.115
  27.7 2.7 %collective-permute-start.7 = (f32[128,8,128]{2,1,0:T(8,128)S(1)}, f32[128,8,128]{2,1,0:T(8,128)S(1)}, u32[]{:S(2)}, u32[]{:S(2)}) collective-permute-start(f32[128,8,128]{2,1,0:T(8,128)S(1)} %get-tuple-element.39), channel_id=1, source_target_pairs={{0,3},{1,0},{2,1},{3,2},{4,196},{5,197},{6,198},{7,199},{8,11},{9,... | collective-permute-start | bytes 1572872 | tf_op jit(solution)/shard_map/ppermute | solution.py:332
  30.4 1.1 %collective-permute-done.1.came.refs_1_ = f32[129,8,128]{2,1,0:T(8,128)S(1)} collective-permute-done((f32[129,8,128]{2,1,0:T(8,128)S(1)}, f32[129,8,128]{2,1,0:T(8,128)S(1)}, u32[]{:S(2)}, u32[]{:S(2)}) %collective-permute-start.1) | collective-permute-done | bytes 528416 | tf_op jit(solution)/shard_map/ppermute | solution.py:332
  31.5 0.1 collective-permute-start.3
  31.6 5.6 %collective-permute-done.6.came.refs_6_ = f32[128,8,128]{2,1,0:T(8,128)S(1)} collective-permute-done((f32[128,8,128]{2,1,0:T(8,128)S(1)}, f32[128,8,128]{2,1,0:T(8,128)S(1)}, u32[]{:S(2)}, u32[]{:S(2)}) %collective-permute-start.6) | collective-permute-done | bytes 524320 | tf_op jit(solution)/shard_map/ppermute | solution.py:332
  37.4 2.7 %collective-permute-start.9 = (f32[64,8,128]{2,1,0:T(8,128)S(1)}, f32[64,8,128]{2,1,0:T(8,128)S(1)}, u32[]{:S(2)}, u32[]{:S(2)}) collective-permute-start(f32[64,8,128]{2,1,0:T(8,128)S(1)} %shard_map.117), channel_id=1, source_target_pairs={{0,3},{1,0},{2,1},{3,2},{4,196},{5,197},{6,198},{7,199},{8,11},{9,... | collective-permute-start | bytes 786440 | tf_op jit(solution)/shard_map/ppermute | solution.py:332
  40.2 0.4 collective-permute-start.4
  40.6 3.2 %collective-permute-done.8.refs_8_ = f32[64,8,128]{2,1,0:T(8,128)S(1)} collective-permute-done((f32[64,8,128]{2,1,0:T(8,128)S(1)}, f32[64,8,128]{2,1,0:T(8,128)S(1)}, u32[]{:S(2)}, u32[]{:S(2)}) %collective-permute-start.8) | collective-permute-done | bytes 262176 | tf_op jit(solution)/shard_map/ppermute | solution.py:332
  43.8 2.5 %collective-permute-done.4.refs_4_ = f32[64,8,128]{2,1,0:T(8,128)S(1)} collective-permute-done((f32[64,8,128]{2,1,0:T(8,128)S(1)}, f32[64,8,128]{2,1,0:T(8,128)S(1)}, u32[]{:S(2)}, u32[]{:S(2)}) %collective-permute-start.4) | collective-permute-done | bytes 262176 | tf_op jit(solution)/shard_map/ppermute | solution.py:332
  46.3 0.2 shard_map.118
  46.5 1.8 %collective-permute-start.10 = (f32[65,8,128]{2,1,0:T(8,128)S(1)}, f32[65,8,128]{2,1,0:T(8,128)S(1)}, u32[]{:S(2)}, u32[]{:S(2)}) collective-permute-start(f32[65,8,128]{2,1,0:T(8,128)S(1)} %get-tuple-element.43), channel_id=1, source_target_pairs={{0,64},{1,65},{2,66},{3,67},{4,5},{5,6},{6,7},{7,4},{8,72},{9,73},... | collective-permute-start | bytes 798728 | tf_op jit(solution)/shard_map/ppermute | solution.py:332
  48.3 1.3 %collective-permute-start.12 = (f32[65,8,128]{2,1,0:T(8,128)S(1)}, f32[65,8,128]{2,1,0:T(8,128)S(1)}, u32[]{:S(2)}, u32[]{:S(2)}) collective-permute-start(f32[65,8,128]{2,1,0:T(8,128)S(1)} %get-tuple-element.45), channel_id=1, source_target_pairs={{0,128},{1,129},{2,130},{3,131},{4,6},{5,7},{6,4},{7,5},{8,136},{9... | collective-permute-start | bytes 798728 | tf_op jit(solution)/shard_map/ppermute | solution.py:332
  49.6 2.2 %collective-permute-done.10.b = f32[65,8,128]{2,1,0:T(8,128)S(1)} collective-permute-done((f32[65,8,128]{2,1,0:T(8,128)S(1)}, f32[65,8,128]{2,1,0:T(8,128)S(1)}, u32[]{:S(2)}, u32[]{:S(2)}) %collective-permute-start.10) | collective-permute-done | bytes 266272 | tf_op jit(solution)/shard_map/ppermute | solution.py:332
  51.8 6.1 %collective-permute-done.11.c = f32[65,8,128]{2,1,0:T(8,128)S(1)} collective-permute-done((f32[65,8,128]{2,1,0:T(8,128)S(1)}, f32[65,8,128]{2,1,0:T(8,128)S(1)}, u32[]{:S(2)}, u32[]{:S(2)}) %collective-permute-start.11) | collective-permute-done | bytes 266272 | tf_op jit(solution)/shard_map/ppermute | solution.py:332
  58.0 25.4 %all_to_all.5.came = f32[16,5,8,128]{3,2,1,0:T(8,128)S(1)} all-to-all(f32[16,5,8,128]{3,2,1,0:T(8,128)S(1)} %bitcast.2), channel_id=1, replica_groups=mesh['dp_0'=4,'dp_1'=8,'dp_2'=2,'outer'=4] {'dp_1','dp_2'}, dimensions={0} | all-to-all | bytes 655360 | tf_op jit(solution)/shard_map/all_to_all | solution.py:417
  83.4 0.6 shard_map.120
  (18 shorter events, 0.5 us)
Async XLA Ops:
  0.6 16.7 %copy-start = (bf16[1024,1024]{1,0:T(8,128)(2,1)S(1)}, bf16[1024,1024]{1,0:T(8,128)(2,1)}, u32[]{:S(2)}) copy-start(bf16[1024,1024]{1,0:T(8,128)(2,1)} %w2.5) | copy-start | bytes 6291460
  16.4 5.1 %collective-permute-start = (f32[513,8,128]{2,1,0:T(8,128)S(1)}, f32[513,8,128]{2,1,0:T(8,128)S(1)}, u32[]{:S(2)}, u32[]{:S(2)}) collective-permute-start(f32[513,8,128]{2,1,0:T(8,128)S(1)} %get-tuple-element.28), channel_id=1, source_target_pairs={{0,4},{4,0},{1,5},{5,1},{2,6},{6,2},{3,7},{7,3},{8,12},{12,8},{9,1... | collective-permute-start | bytes 6303752 | tf_op jit(solution)/shard_map/ppermute | solution.py:402
  20.0 7.3 %collective-permute-start.5 = (f32[512,8,128]{2,1,0:T(8,128)S(1)}, f32[512,8,128]{2,1,0:T(8,128)S(1)}, u32[]{:S(2)}, u32[]{:S(2)}) collective-permute-start(f32[512,8,128]{2,1,0:T(8,128)S(1)} %first_grad.3), channel_id=1, source_target_pairs={{0,4},{4,0},{1,5},{5,1},{2,6},{6,2},{3,7},{7,3},{8,12},{12,8},{9,1... | collective-permute-start | bytes 6291464 | tf_op jit(solution)/shard_map/ppermute | solution.py:402
  21.8 9.7 %collective-permute-start.1 = (f32[129,8,128]{2,1,0:T(8,128)S(1)}, f32[129,8,128]{2,1,0:T(8,128)S(1)}, u32[]{:S(2)}, u32[]{:S(2)}) collective-permute-start(f32[129,8,128]{2,1,0:T(8,128)S(1)} %get-tuple-element.31), channel_id=1, source_target_pairs={{0,1},{1,2},{2,3},{3,0},{4,68},{5,69},{6,70},{7,71},{8,9},{9,10},{... | collective-permute-start | bytes 1585160 | tf_op jit(solution)/shard_map/ppermute | solution.py:332
  23.2 17.0 %collective-permute-start.2 = (f32[129,8,128]{2,1,0:T(8,128)S(1)}, f32[129,8,128]{2,1,0:T(8,128)S(1)}, u32[]{:S(2)}, u32[]{:S(2)}) collective-permute-start(f32[129,8,128]{2,1,0:T(8,128)S(1)} %get-tuple-element.32), channel_id=1, source_target_pairs={{0,3},{1,0},{2,1},{3,2},{4,196},{5,197},{6,198},{7,199},{8,11},{9,... | collective-permute-start | bytes 1585160 | tf_op jit(solution)/shard_map/ppermute | solution.py:332
  27.6 9.6 %collective-permute-start.6 = (f32[128,8,128]{2,1,0:T(8,128)S(1)}, f32[128,8,128]{2,1,0:T(8,128)S(1)}, u32[]{:S(2)}, u32[]{:S(2)}) collective-permute-start(f32[128,8,128]{2,1,0:T(8,128)S(1)} %get-tuple-element.38), channel_id=1, source_target_pairs={{0,1},{1,2},{2,3},{3,0},{4,68},{5,69},{6,70},{7,71},{8,9},{9,10},{... | collective-permute-start | bytes 1572872 | tf_op jit(solution)/shard_map/ppermute | solution.py:332
  27.7 9.6 %collective-permute-start.7 = (f32[128,8,128]{2,1,0:T(8,128)S(1)}, f32[128,8,128]{2,1,0:T(8,128)S(1)}, u32[]{:S(2)}, u32[]{:S(2)}) collective-permute-start(f32[128,8,128]{2,1,0:T(8,128)S(1)} %get-tuple-element.39), channel_id=1, source_target_pairs={{0,3},{1,0},{2,1},{3,2},{4,196},{5,197},{6,198},{7,199},{8,11},{9,... | collective-permute-start | bytes 1572872 | tf_op jit(solution)/shard_map/ppermute | solution.py:332
  31.5 14.7 %collective-permute-start.3 = (f32[65,8,128]{2,1,0:T(8,128)S(1)}, f32[65,8,128]{2,1,0:T(8,128)S(1)}, u32[]{:S(2)}, u32[]{:S(2)}) collective-permute-start(f32[65,8,128]{2,1,0:T(8,128)S(1)} %shard_map.113), channel_id=1, source_target_pairs={{0,1},{1,2},{2,3},{3,0},{4,68},{5,69},{6,70},{7,71},{8,9},{9,10},{... | collective-permute-start | bytes 798728 | tf_op jit(solution)/shard_map/ppermute | solution.py:332
  37.3 6.5 %collective-permute-start.8 = (f32[64,8,128]{2,1,0:T(8,128)S(1)}, f32[64,8,128]{2,1,0:T(8,128)S(1)}, u32[]{:S(2)}, u32[]{:S(2)}) collective-permute-start(f32[64,8,128]{2,1,0:T(8,128)S(1)} %shard_map.116), channel_id=1, source_target_pairs={{0,1},{1,2},{2,3},{3,0},{4,68},{5,69},{6,70},{7,71},{8,9},{9,10},{... | collective-permute-start | bytes 786440 | tf_op jit(solution)/shard_map/ppermute | solution.py:332
  37.4 6.4 %collective-permute-start.9 = (f32[64,8,128]{2,1,0:T(8,128)S(1)}, f32[64,8,128]{2,1,0:T(8,128)S(1)}, u32[]{:S(2)}, u32[]{:S(2)}) collective-permute-start(f32[64,8,128]{2,1,0:T(8,128)S(1)} %shard_map.117), channel_id=1, source_target_pairs={{0,3},{1,0},{2,1},{3,2},{4,196},{5,197},{6,198},{7,199},{8,11},{9,... | collective-permute-start | bytes 786440 | tf_op jit(solution)/shard_map/ppermute | solution.py:332
  40.2 6.1 %collective-permute-start.4 = (f32[64,8,128]{2,1,0:T(8,128)S(1)}, f32[64,8,128]{2,1,0:T(8,128)S(1)}, u32[]{:S(2)}, u32[]{:S(2)}) collective-permute-start(f32[64,8,128]{2,1,0:T(8,128)S(1)} %shard_map.114), channel_id=1, source_target_pairs={{0,3},{1,0},{2,1},{3,2},{4,196},{5,197},{6,198},{7,199},{8,11},{9,... | collective-permute-start | bytes 786440 | tf_op jit(solution)/shard_map/ppermute | solution.py:332
  46.5 5.3 %collective-permute-start.10 = (f32[65,8,128]{2,1,0:T(8,128)S(1)}, f32[65,8,128]{2,1,0:T(8,128)S(1)}, u32[]{:S(2)}, u32[]{:S(2)}) collective-permute-start(f32[65,8,128]{2,1,0:T(8,128)S(1)} %get-tuple-element.43), channel_id=1, source_target_pairs={{0,64},{1,65},{2,66},{3,67},{4,5},{5,6},{6,7},{7,4},{8,72},{9,73},... | collective-permute-start | bytes 798728 | tf_op jit(solution)/shard_map/ppermute | solution.py:332
  48.3 9.6 %collective-permute-start.11 = (f32[65,8,128]{2,1,0:T(8,128)S(1)}, f32[65,8,128]{2,1,0:T(8,128)S(1)}, u32[]{:S(2)}, u32[]{:S(2)}) collective-permute-start(f32[65,8,128]{2,1,0:T(8,128)S(1)} %get-tuple-element.44), channel_id=1, source_target_pairs={{0,192},{1,193},{2,194},{3,195},{4,7},{5,4},{6,5},{7,6},{8,200},{9... | collective-permute-start | bytes 798728 | tf_op jit(solution)/shard_map/ppermute | solution.py:332
  48.3 9.6 %collective-permute-start.12 = (f32[65,8,128]{2,1,0:T(8,128)S(1)}, f32[65,8,128]{2,1,0:T(8,128)S(1)}, u32[]{:S(2)}, u32[]{:S(2)}) collective-permute-start(f32[65,8,128]{2,1,0:T(8,128)S(1)} %get-tuple-element.45), channel_id=1, source_target_pairs={{0,128},{1,129},{2,130},{3,131},{4,6},{5,7},{6,4},{7,5},{8,136},{9... | collective-permute-start | bytes 798728 | tf_op jit(solution)/shard_map/ppermute | solution.py:332

commit v2 on v1

--- a/solution.py
+++ b/solution.py
@@ -341,41 +341,44 @@
     return own, came_up, came_down, up, down
 
 
-def plane_sum_kernel(*refs):
-    second, first, pieces = refs[:5], refs[5:10], refs[10:]
+def plane_sum_kernel(own, came_up, came_down, up, down, *pieces):
     for k in range(4):
         q = along(False, k)
-        for g, (own, came_up, came_down, up, down) in enumerate((second, first)):
-            here = pl.multiple_of(q * 32, 32)
-            there = pl.multiple_of(q * 16, 16)
-            pieces[k][pl.ds(g * 32, 16)] = own[pl.ds(here, 16)] + up[pl.ds(there, 16)] + came_down[pl.ds(64 + there, 16)]
-            pieces[k][pl.ds(g * 32 + 16, 16)] = own[pl.ds(here + 16, 16)] + came_up[pl.ds(64 + there, 16)] + down[pl.ds(there, 16)]
-        pieces[k][64] = second[0][128] + second[3][64] + second[2][128]
-
-
-def plane_sum(second, first):
-    return call(plane_sum_kernel, (tiles(65),) * 4, (*second, *first), 10, 2**20, 5 * 2**20)
+        here = pl.multiple_of(q * 32, 32)
+        there = pl.multiple_of(q * 16, 16)
+        pieces[k][pl.ds(0, 16)] = own[pl.ds(here, 16)] + up[pl.ds(there, 16)] + came_down[pl.ds(64 + there, 16)]
+        pieces[k][pl.ds(16, 16)] = own[pl.ds(here + 16, 16)] + came_up[pl.ds(64 + there, 16)] + down[pl.ds(there, 16)]
+        if own.shape[0] > 128:
+            pieces[k][32] = own[128] + up[64] + came_down[128]
+
+
+def plane_sum(ins):
+    return call(plane_sum_kernel, (tiles(ins[0].shape[0] - 96),) * 4, tuple(ins), 6, 2**19, 5 * 2**19)
 
 
 def exchange(pieces, x_on_core):
-    return [pieces[0]] + [shift(pieces[k], k, x_on_core) for k in (1, 3, 2)]
-
-
-def line_sum_kernel(a, b, c, d, out):
-    for g in range(2):
+    came = [pieces[0]]
+    for k in (1, 3, 2):
+        came.append(shift(pieces[k], k, x_on_core))
+    return came
+
+
+def line_sum_kernel(*refs):
+    second, first, out = refs[:4], refs[4:8], refs[8]
+    for g, (a, b, c, d) in enumerate((second, first)):
         for t in range(2):
             for core in range(2):
-                at = pl.ds(g * 32 + t * 16 + core * 8, 8)
+                at = pl.ds(t * 16 + core * 8, 8)
                 out[:, core, 2 * g + t] = (a[at] + b[at]) + (c[at] + d[at])
-    bucket = (a[64] + b[64]) + (c[64] + d[64])
+    bucket = (second[0][32] + second[1][32]) + (second[2][32] + second[3][32])
     for z in range(8):
         for core in range(2):
             out[z, core, 4] = bucket
 
 
-def line_sum(pieces):
+def line_sum(second, first):
     outs = (jax.ShapeDtypeStruct((8, 2, 5, 8, 128), F32),)
-    return call(line_sum_kernel, outs, tuple(pieces), 4, 2**18, 2**20)[0]
+    return call(line_sum_kernel, outs, (*second, *first), 4, 2**18, 2**20)[0]
 
 
 def last_sum_kernel(came, first, second, bucket):
@@ -413,8 +416,9 @@
     second = around(*core_sum(keep_s, came_s, bucket))
     keep_f = first_grad(grad_out, pre_hi, inputs, w_second, False)
     first = around(*core_sum(keep_f, came_f))
-    pieces = exchange(plane_sum(second, first), 1)
-    came = lax.all_to_all(line_sum(pieces).reshape(16, 5, 8, 128), ("dp_1", "dp_2"), 0, 0, tiled=True)
+    second = exchange(plane_sum(second), 1)
+    first = exchange(plane_sum(first), 1)
+    came = lax.all_to_all(line_sum(second, first).reshape(16, 5, 8, 128), ("dp_1", "dp_2"), 0, 0, tiled=True)
     first_rows, second_rows, losses = last_sum(came)
     return first_rows, second_rows, losses.reshape(BUCKETS)
 

time: 84.1 us -> 85.5 us (1.017)
  the two profiles are of different devices: /device:TPU:7 before, /device:TPU:1 now
where the time goes in v2:
time: 85.5 us; the launch traced here: 85.4 us
  blocking collectives  26.2 us (31%)
  Pallas kernels  24.1 us (28%)
  starting transfers between devices  20.6 us (24%)
  waiting for transfers between devices  13.6 us (16%)
    all_to_all x1, blocking collectives, step(): lax.all_to_all(line_sum(second, first).reshape(16, 5, 8, 128), ('dp_1', '...  26.2 us
    ppermute x14, starting transfers between devices, shift(): return lax.ppermute(piece, DP_OUTER, shift_pairs(k, x_on_core))  17.1 us
    pallas_call x1, Pallas kernels, forward(): pl.pallas_call(functools.partial(forward_kernel, total=total), out_shape=...  15.7 us
    ppermute x14, waiting for transfers between devices, shift(): return lax.ppermute(piece, DP_OUTER, shift_pairs(k, x_on_core))  12.6 us
    pallas_call x2, Pallas kernels, first_grad(): pl.pallas_call(functools.partial(first_kernel, color_flip=color_flip), ou...  5.59 us
    ppermute x2, starting transfers between devices, other_core(): return lax.ppermute(array, 'dp_2', [(0, 1), (1, 0)])  3.44 us
  transfers between devices with their start and end apart: 16, of which 7 were waited for; matrix products, arithmetic and copies ran while one was open for 0% of the time, Pallas kernels for 6%

profile of v2, /device:TPU:1, one launch (start us, length us, event | category | flops | bytes accessed | tf_op | source)
XLA Modules:
  0.0 85.4 jit_solution(270936238415987563)
XLA Ops:
  0.6 15.7 %forward.1 = (f32[513,8,128]{2,1,0:T(8,128)S(1)}, f32[8,128]{1,0:T(8,128)S(1)}, bf16[896,1024]{1,0:T(8,128)(2,1)S(1)}, f32[896,1024]{1,0:T(8,128)S(1)}, bf16[896...) custom-call(s32[8]{0:T(128)} %t_index_hbm.1, s32[8]{0:T(128)} %bucket_id_hbm.1, s32[16]{0:T(128)} %bucket_count_hbm.1, ...), custom_call_target="tpu_custom_call" | custom-call | flops 8455716864 | bytes 25165824 | tf_op jit(solution)/shard_map/forward/pallas_call | solution.py:224
  16.4 2.9 %first_grad.3 = f32[512,8,128]{2,1,0:T(8,128)S(1)} custom-call(bf16[896,1024]{1,0:T(8,128)(2,1)S(1)} %get-tuple-element.31.grad_out, f32[896,1024]{1,0:T(8,128)S(1)} %get-tuple-element.43.pre_hi, bf16[896,1024]{1,0:T(8,128)(2,1)S(1)} %get-tuple-element.44.inputs, bf16[1024,1024]{1,0:T(8,128)(2,1)S(1)} %copy-done), custom_call_target="tpu_custom_call" | custom-call | flops 1879048192 | bytes 8388608 | tf_op jit(solution)/shard_map/first_grad/pallas_call | solution.py:254
  19.3 3.3 %collective-permute-start.8 = (f32[512,8,128]{2,1,0:T(8,128)S(1)}, f32[512,8,128]{2,1,0:T(8,128)S(1)}, u32[]{:S(2)}, u32[]{:S(2)}) collective-permute-start(f32[512,8,128]{2,1,0:T(8,128)S(1)} %first_grad.3), channel_id=1, source_target_pairs={{0,4},{4,0},{1,5},{5,1},{2,6},{6,2},{3,7},{7,3},{8,12},{12,8},{9,1... | collective-permute-start | bytes 6291464 | tf_op jit(solution)/shard_map/ppermute | solution.py:405
  22.7 2.7 %first_grad.2.keep = f32[512,8,128]{2,1,0:T(8,128)S(1)} custom-call(bf16[896,1024]{1,0:T(8,128)(2,1)S(1)} %get-tuple-element.31.grad_out, f32[896,1024]{1,0:T(8,128)S(1)} %get-tuple-element.43.pre_hi, bf16[896,1024]{1,0:T(8,128)(2,1)S(1)} %get-tuple-element.44.inputs, bf16[1024,1024]{1,0:T(8,128)(2,1)S(1)} %copy-done), custom_call_target="tpu_custom_call" | custom-call | flops 1879048192 | bytes 8388608 | tf_op jit(solution)/shard_map/first_grad/pallas_call | solution.py:254
  25.4 1.0 %collective-permute-done.8.came = f32[512,8,128]{2,1,0:T(8,128)S(1)} collective-permute-done((f32[512,8,128]{2,1,0:T(8,128)S(1)}, f32[512,8,128]{2,1,0:T(8,128)S(1)}, u32[]{:S(2)}, u32[]{:S(2)}) %collective-permute-start.8) | collective-permute-done | bytes 2097184 | tf_op jit(solution)/shard_map/ppermute | solution.py:405
  26.4 0.2 shard_map.116
  26.7 2.7 %collective-permute-start.10 = (f32[128,8,128]{2,1,0:T(8,128)S(1)}, f32[128,8,128]{2,1,0:T(8,128)S(1)}, u32[]{:S(2)}, u32[]{:S(2)}) collective-permute-start(f32[128,8,128]{2,1,0:T(8,128)S(1)} %get-tuple-element.47), channel_id=1, source_target_pairs={{0,3},{1,0},{2,1},{3,2},{4,196},{5,197},{6,198},{7,199},{8,11},{9,... | collective-permute-start | bytes 1572872 | tf_op jit(solution)/shard_map/ppermute | solution.py:332
  29.4 1.4 %second_grad.1.keep = f32[512,8,128]{2,1,0:T(8,128)S(1)} custom-call(bf16[896,1024]{1,0:T(8,128)(2,1)S(1)} %get-tuple-element.30.act_hi, bf16[896,1024]{1,0:T(8,128)(2,1)S(1)} %get-tuple-element.31.grad_out), custom_call_target="tpu_custom_call" | custom-call | flops 939524096 | bytes 4194304 | tf_op jit(solution)/shard_map/second_grad/pallas_call | solution.py:242
  30.8 0.2 shard_map.112
  31.1 2.7 %collective-permute-start.2 = (f32[129,8,128]{2,1,0:T(8,128)S(1)}, f32[129,8,128]{2,1,0:T(8,128)S(1)}, u32[]{:S(2)}, u32[]{:S(2)}) collective-permute-start(f32[129,8,128]{2,1,0:T(8,128)S(1)} %get-tuple-element.36), channel_id=1, source_target_pairs={{0,3},{1,0},{2,1},{3,2},{4,196},{5,197},{6,198},{7,199},{8,11},{9,... | collective-permute-start | bytes 1585160 | tf_op jit(solution)/shard_map/ppermute | solution.py:332
  33.8 2.5 %collective-permute-done.9.came.came_up = f32[128,8,128]{2,1,0:T(8,128)S(1)} collective-permute-done((f32[128,8,128]{2,1,0:T(8,128)S(1)}, f32[128,8,128]{2,1,0:T(8,128)S(1)}, u32[]{:S(2)}, u32[]{:S(2)}) %collective-permute-start.9) | collective-permute-done | bytes 524320 | tf_op jit(solution)/shard_map/ppermute | solution.py:332
  36.4 2.7 %collective-permute-start.12 = (f32[64,8,128]{2,1,0:T(8,128)S(1)}, f32[64,8,128]{2,1,0:T(8,128)S(1)}, u32[]{:S(2)}, u32[]{:S(2)}) collective-permute-start(f32[64,8,128]{2,1,0:T(8,128)S(1)} %shard_map.118), channel_id=1, source_target_pairs={{0,3},{1,0},{2,1},{3,2},{4,196},{5,197},{6,198},{7,199},{8,11},{9,... | collective-permute-start | bytes 786440 | tf_op jit(solution)/shard_map/ppermute | solution.py:332
  39.1 2.8 %collective-permute-done.1.came.came_up = f32[129,8,128]{2,1,0:T(8,128)S(1)} collective-permute-done((f32[129,8,128]{2,1,0:T(8,128)S(1)}, f32[129,8,128]{2,1,0:T(8,128)S(1)}, u32[]{:S(2)}, u32[]{:S(2)}) %collective-permute-start.1) | collective-permute-done | bytes 528416 | tf_op jit(solution)/shard_map/ppermute | solution.py:332
  42.1 2.7 %collective-permute-start.4 = (f32[64,8,128]{2,1,0:T(8,128)S(1)}, f32[64,8,128]{2,1,0:T(8,128)S(1)}, u32[]{:S(2)}, u32[]{:S(2)}) collective-permute-start(f32[64,8,128]{2,1,0:T(8,128)S(1)} %shard_map.114), channel_id=1, source_target_pairs={{0,3},{1,0},{2,1},{3,2},{4,196},{5,197},{6,198},{7,199},{8,11},{9,... | collective-permute-start | bytes 786440 | tf_op jit(solution)/shard_map/ppermute | solution.py:332
  44.9 0.3 collective-permute-start.13
  45.2 2.9 %collective-permute-done.4.down = f32[64,8,128]{2,1,0:T(8,128)S(1)} collective-permute-done((f32[64,8,128]{2,1,0:T(8,128)S(1)}, f32[64,8,128]{2,1,0:T(8,128)S(1)}, u32[]{:S(2)}, u32[]{:S(2)}) %collective-permute-start.4) | collective-permute-done | bytes 262176 | tf_op jit(solution)/shard_map/ppermute | solution.py:332
  48.1 0.7 collective-permute-done.3.up
  49.0 2.7 %collective-permute-start.6 = (f32[33,8,128]{2,1,0:T(8,128)S(1)}, f32[33,8,128]{2,1,0:T(8,128)S(1)}, u32[]{:S(2)}, u32[]{:S(2)}) collective-permute-start(f32[33,8,128]{2,1,0:T(8,128)S(1)} %get-tuple-element.41), channel_id=1, source_target_pairs={{0,192},{1,193},{2,194},{3,195},{4,7},{5,4},{6,5},{7,6},{8,200},{9... | collective-permute-start | bytes 405512 | tf_op jit(solution)/shard_map/ppermute | solution.py:332
  51.6 1.3 %collective-permute-start.14 = (f32[32,8,128]{2,1,0:T(8,128)S(1)}, f32[32,8,128]{2,1,0:T(8,128)S(1)}, u32[]{:S(2)}, u32[]{:S(2)}) collective-permute-start(f32[32,8,128]{2,1,0:T(8,128)S(1)} %get-tuple-element.52), channel_id=1, source_target_pairs={{0,192},{1,193},{2,194},{3,195},{4,7},{5,4},{6,5},{7,6},{8,200},{9... | collective-permute-start | bytes 393224 | tf_op jit(solution)/shard_map/ppermute | solution.py:332
  52.9 1.7 %collective-permute-start.15 = (f32[32,8,128]{2,1,0:T(8,128)S(1)}, f32[32,8,128]{2,1,0:T(8,128)S(1)}, u32[]{:S(2)}, u32[]{:S(2)}) collective-permute-start(f32[32,8,128]{2,1,0:T(8,128)S(1)} %get-tuple-element.53), channel_id=1, source_target_pairs={{0,128},{1,129},{2,130},{3,131},{4,6},{5,7},{6,4},{7,5},{8,136},{9... | collective-permute-start | bytes 393224 | tf_op jit(solution)/shard_map/ppermute | solution.py:332
  54.6 3.2 %collective-permute-done.14.refs_6_ = f32[32,8,128]{2,1,0:T(8,128)S(1)} collective-permute-done((f32[32,8,128]{2,1,0:T(8,128)S(1)}, f32[32,8,128]{2,1,0:T(8,128)S(1)}, u32[]{:S(2)}, u32[]{:S(2)}) %collective-permute-start.14) | collective-permute-done | bytes 131104 | tf_op jit(solution)/shard_map/ppermute | solution.py:332
  57.9 0.6 collective-permute-done.15.refs_7_
  58.5 26.2 %all_to_all.5.came = f32[16,5,8,128]{3,2,1,0:T(8,128)S(1)} all-to-all(f32[16,5,8,128]{3,2,1,0:T(8,128)S(1)} %bitcast.2), channel_id=1, replica_groups=mesh['dp_0'=4,'dp_1'=8,'dp_2'=2,'outer'=4] {'dp_1','dp_2'}, dimensions={0} | all-to-all | bytes 655360 | tf_op jit(solution)/shard_map/all_to_all | solution.py:421
  84.7 0.6 shard_map.121
  (25 shorter events, 0.9 us)
Async XLA Ops:
  0.6 15.7 %copy-start = (bf16[1024,1024]{1,0:T(8,128)(2,1)S(1)}, bf16[1024,1024]{1,0:T(8,128)(2,1)}, u32[]{:S(2)}) copy-start(bf16[1024,1024]{1,0:T(8,128)(2,1)} %w2.5) | copy-start | bytes 6291460
  19.3 7.1 %collective-permute-start.8 = (f32[512,8,128]{2,1,0:T(8,128)S(1)}, f32[512,8,128]{2,1,0:T(8,128)S(1)}, u32[]{:S(2)}, u32[]{:S(2)}) collective-permute-start(f32[512,8,128]{2,1,0:T(8,128)S(1)} %first_grad.3), channel_id=1, source_target_pairs={{0,4},{4,0},{1,5},{5,1},{2,6},{6,2},{3,7},{7,3},{8,12},{12,8},{9,1... | collective-permute-start | bytes 6291464 | tf_op jit(solution)/shard_map/ppermute | solution.py:405
  22.6 8.1 %collective-permute-start = (f32[513,8,128]{2,1,0:T(8,128)S(1)}, f32[513,8,128]{2,1,0:T(8,128)S(1)}, u32[]{:S(2)}, u32[]{:S(2)}) collective-permute-start(f32[513,8,128]{2,1,0:T(8,128)S(1)} %get-tuple-element.32), channel_id=1, source_target_pairs={{0,4},{4,0},{1,5},{5,1},{2,6},{6,2},{3,7},{7,3},{8,12},{12,8},{9,1... | collective-permute-start | bytes 6303752 | tf_op jit(solution)/shard_map/ppermute | solution.py:405
  26.6 9.6 %collective-permute-start.9 = (f32[128,8,128]{2,1,0:T(8,128)S(1)}, f32[128,8,128]{2,1,0:T(8,128)S(1)}, u32[]{:S(2)}, u32[]{:S(2)}) collective-permute-start(f32[128,8,128]{2,1,0:T(8,128)S(1)} %get-tuple-element.46), channel_id=1, source_target_pairs={{0,1},{1,2},{2,3},{3,0},{4,68},{5,69},{6,70},{7,71},{8,9},{9,10},{... | collective-permute-start | bytes 1572872 | tf_op jit(solution)/shard_map/ppermute | solution.py:332
  26.7 9.6 %collective-permute-start.10 = (f32[128,8,128]{2,1,0:T(8,128)S(1)}, f32[128,8,128]{2,1,0:T(8,128)S(1)}, u32[]{:S(2)}, u32[]{:S(2)}) collective-permute-start(f32[128,8,128]{2,1,0:T(8,128)S(1)} %get-tuple-element.47), channel_id=1, source_target_pairs={{0,3},{1,0},{2,1},{3,2},{4,196},{5,197},{6,198},{7,199},{8,11},{9,... | collective-permute-start | bytes 1572872 | tf_op jit(solution)/shard_map/ppermute | solution.py:332
  31.0 10.9 %collective-permute-start.1 = (f32[129,8,128]{2,1,0:T(8,128)S(1)}, f32[129,8,128]{2,1,0:T(8,128)S(1)}, u32[]{:S(2)}, u32[]{:S(2)}) collective-permute-start(f32[129,8,128]{2,1,0:T(8,128)S(1)} %get-tuple-element.35), channel_id=1, source_target_pairs={{0,1},{1,2},{2,3},{3,0},{4,68},{5,69},{6,70},{7,71},{8,9},{9,10},{... | collective-permute-start | bytes 1585160 | tf_op jit(solution)/shard_map/ppermute | solution.py:332
  31.1 10.9 %collective-permute-start.2 = (f32[129,8,128]{2,1,0:T(8,128)S(1)}, f32[129,8,128]{2,1,0:T(8,128)S(1)}, u32[]{:S(2)}, u32[]{:S(2)}) collective-permute-start(f32[129,8,128]{2,1,0:T(8,128)S(1)} %get-tuple-element.36), channel_id=1, source_target_pairs={{0,3},{1,0},{2,1},{3,2},{4,196},{5,197},{6,198},{7,199},{8,11},{9,... | collective-permute-start | bytes 1585160 | tf_op jit(solution)/shard_map/ppermute | solution.py:332
  36.3 8.5 %collective-permute-start.11 = (f32[64,8,128]{2,1,0:T(8,128)S(1)}, f32[64,8,128]{2,1,0:T(8,128)S(1)}, u32[]{:S(2)}, u32[]{:S(2)}) collective-permute-start(f32[64,8,128]{2,1,0:T(8,128)S(1)} %shard_map.117), channel_id=1, source_target_pairs={{0,1},{1,2},{2,3},{3,0},{4,68},{5,69},{6,70},{7,71},{8,9},{9,10},{... | collective-permute-start | bytes 786440 | tf_op jit(solution)/shard_map/ppermute | solution.py:332
  36.4 8.4 %collective-permute-start.12 = (f32[64,8,128]{2,1,0:T(8,128)S(1)}, f32[64,8,128]{2,1,0:T(8,128)S(1)}, u32[]{:S(2)}, u32[]{:S(2)}) collective-permute-start(f32[64,8,128]{2,1,0:T(8,128)S(1)} %shard_map.118), channel_id=1, source_target_pairs={{0,3},{1,0},{2,1},{3,2},{4,196},{5,197},{6,198},{7,199},{8,11},{9,... | collective-permute-start | bytes 786440 | tf_op jit(solution)/shard_map/ppermute | solution.py:332
  41.9 6.8 %collective-permute-start.3 = (f32[65,8,128]{2,1,0:T(8,128)S(1)}, f32[65,8,128]{2,1,0:T(8,128)S(1)}, u32[]{:S(2)}, u32[]{:S(2)}) collective-permute-start(f32[65,8,128]{2,1,0:T(8,128)S(1)} %shard_map.113), channel_id=1, source_target_pairs={{0,1},{1,2},{2,3},{3,0},{4,68},{5,69},{6,70},{7,71},{8,9},{9,10},{... | collective-permute-start | bytes 798728 | tf_op jit(solution)/shard_map/ppermute | solution.py:332
  42.1 6.0 %collective-permute-start.4 = (f32[64,8,128]{2,1,0:T(8,128)S(1)}, f32[64,8,128]{2,1,0:T(8,128)S(1)}, u32[]{:S(2)}, u32[]{:S(2)}) collective-permute-start(f32[64,8,128]{2,1,0:T(8,128)S(1)} %shard_map.114), channel_id=1, source_target_pairs={{0,3},{1,0},{2,1},{3,2},{4,196},{5,197},{6,198},{7,199},{8,11},{9,... | collective-permute-start | bytes 786440 | tf_op jit(solution)/shard_map/ppermute | solution.py:332
  44.9 8.0 %collective-permute-start.13 = (f32[32,8,128]{2,1,0:T(8,128)S(1)}, f32[32,8,128]{2,1,0:T(8,128)S(1)}, u32[]{:S(2)}, u32[]{:S(2)}) collective-permute-start(f32[32,8,128]{2,1,0:T(8,128)S(1)} %get-tuple-element.51), channel_id=1, source_target_pairs={{0,64},{1,65},{2,66},{3,67},{4,5},{5,6},{6,7},{7,4},{8,72},{9,73},... | collective-permute-start | bytes 393224 | tf_op jit(solution)/shard_map/ppermute | solution.py:332
  48.9 9.5 %collective-permute-start.5 = (f32[33,8,128]{2,1,0:T(8,128)S(1)}, f32[33,8,128]{2,1,0:T(8,128)S(1)}, u32[]{:S(2)}, u32[]{:S(2)}) collective-permute-start(f32[33,8,128]{2,1,0:T(8,128)S(1)} %get-tuple-element.40), channel_id=1, source_target_pairs={{0,64},{1,65},{2,66},{3,67},{4,5},{5,6},{6,7},{7,4},{8,72},{9,73},... | collective-permute-start | bytes 405512 | tf_op jit(solution)/shard_map/ppermute | solution.py:332
  49.0 9.4 %collective-permute-start.6 = (f32[33,8,128]{2,1,0:T(8,128)S(1)}, f32[33,8,128]{2,1,0:T(8,128)S(1)}, u32[]{:S(2)}, u32[]{:S(2)}) collective-permute-start(f32[33,8,128]{2,1,0:T(8,128)S(1)} %get-tuple-element.41), channel_id=1, source_target_pairs={{0,192},{1,193},{2,194},{3,195},{4,7},{5,4},{6,5},{7,6},{8,200},{9... | collective-permute-start | bytes 405512 | tf_op jit(solution)/shard_map/ppermute | solution.py:332
  51.6 6.8 %collective-permute-start.7 = (f32[33,8,128]{2,1,0:T(8,128)S(1)}, f32[33,8,128]{2,1,0:T(8,128)S(1)}, u32[]{:S(2)}, u32[]{:S(2)}) collective-permute-start(f32[33,8,128]{2,1,0:T(8,128)S(1)} %get-tuple-element.42), channel_id=1, source_target_pairs={{0,128},{1,129},{2,130},{3,131},{4,6},{5,7},{6,4},{7,5},{8,136},{9... | collective-permute-start | bytes 405512 | tf_op jit(solution)/shard_map/ppermute | solution.py:332
  51.6 6.2 %collective-permute-start.14 = (f32[32,8,128]{2,1,0:T(8,128)S(1)}, f32[32,8,128]{2,1,0:T(8,128)S(1)}, u32[]{:S(2)}, u32[]{:S(2)}) collective-permute-start(f32[32,8,128]{2,1,0:T(8,128)S(1)} %get-tuple-element.52), channel_id=1, source_target_pairs={{0,192},{1,193},{2,194},{3,195},{4,7},{5,4},{6,5},{7,6},{8,200},{9... | collective-permute-start | bytes 393224 | tf_op jit(solution)/shard_map/ppermute | solution.py:332
  52.9 5.5 %collective-permute-start.15 = (f32[32,8,128]{2,1,0:T(8,128)S(1)}, f32[32,8,128]{2,1,0:T(8,128)S(1)}, u32[]{:S(2)}, u32[]{:S(2)}) collective-permute-start(f32[32,8,128]{2,1,0:T(8,128)S(1)} %get-tuple-element.53), channel_id=1, source_target_pairs={{0,128},{1,129},{2,130},{3,131},{4,6},{5,7},{6,4},{7,5},{8,136},{9... | collective-permute-start | bytes 393224 | tf_op jit(solution)/shard_map/ppermute | solution.py:332

commit v3 on v1

--- a/solution.py
+++ b/solution.py
@@ -333,7 +333,8 @@
 
 
 def around(own, up, down, up_kept, down_kept):
-    came_up, came_down = shift(up, 1, 0), shift(down, 3, 0)
+    came_up = shift(up, 1, 0)
+    came_down = shift(down, 3, 0)
     up = middle_sum(came_up, up_kept)
     up = shift(up, 1, 0)
     down = middle_sum(came_down, down_kept)
@@ -358,7 +359,7 @@
 
 
 def exchange(pieces, x_on_core):
-    return [pieces[0]] + [shift(pieces[k], k, x_on_core) for k in (1, 3, 2)]
+    return [pieces[0]] + [shift(pieces[k], k, x_on_core) for k in (2, 1, 3)]
 
 
 def line_sum_kernel(a, b, c, d, out):

time: 84.1 us -> 83.5 us (level)
  transfers between devices with their start and end apart: 13 -> 13, of which waited for: 6 -> 7; matrix products, arithmetic and copies ran while one was open for 0% -> 0% of each run, Pallas kernels for 9% -> 9%
where the time goes in v3:
time: 83.5 us; the launch traced here: 83.4 us
  blocking collectives  25.9 us (31%)
  Pallas kernels  24 us (29%)
  waiting for transfers between devices  20 us (24%)
  starting transfers between devices  12.8 us (15%)
    all_to_all x1, blocking collectives, step(): lax.all_to_all(line_sum(pieces).reshape(16, 5, 8, 128), ('dp_1', 'dp_2'),...  25.9 us
    ppermute x11, waiting for transfers between devices, shift(): return lax.ppermute(piece, DP_OUTER, shift_pairs(k, x_on_core))  20 us
    pallas_call x1, Pallas kernels, forward(): pl.pallas_call(functools.partial(forward_kernel, total=total), out_shape=...  15.7 us
    ppermute x11, starting transfers between devices, shift(): return lax.ppermute(piece, DP_OUTER, shift_pairs(k, x_on_core))  11.7 us
    pallas_call x2, Pallas kernels, first_grad(): pl.pallas_call(functools.partial(first_kernel, color_flip=color_flip), ou...  5.38 us
  transfers between devices with their start and end apart: 13, of which 7 were waited for; matrix products, arithmetic and copies ran while one was open for 0% of the time, Pallas kernels for 9%

profile of v3, /device:TPU:7, one launch (start us, length us, event | category | flops | bytes accessed | tf_op | source)
XLA Modules:
  0.0 83.4 jit_solution(6388895984543588687)
XLA Ops:
  0.6 15.7 %forward.1 = (f32[513,8,128]{2,1,0:T(8,128)S(1)}, f32[8,128]{1,0:T(8,128)S(1)}, bf16[896,1024]{1,0:T(8,128)(2,1)S(1)}, f32[896,1024]{1,0:T(8,128)S(1)}, bf16[896...) custom-call(s32[8]{0:T(128)} %t_index_hbm.1, s32[8]{0:T(128)} %bucket_id_hbm.1, s32[16]{0:T(128)} %bucket_count_hbm.1, ...), custom_call_target="tpu_custom_call" | custom-call | flops 8455716864 | bytes 25165824 | tf_op jit(solution)/shard_map/forward/pallas_call | solution.py:224
  16.4 1.0 %collective-permute-start = (f32[513,8,128]{2,1,0:T(8,128)S(1)}, f32[513,8,128]{2,1,0:T(8,128)S(1)}, u32[]{:S(2)}, u32[]{:S(2)}) collective-permute-start(f32[513,8,128]{2,1,0:T(8,128)S(1)} %get-tuple-element.28), channel_id=1, source_target_pairs={{0,4},{4,0},{1,5},{5,1},{2,6},{6,2},{3,7},{7,3},{8,12},{12,8},{9,1... | collective-permute-start | bytes 6303752 | tf_op jit(solution)/shard_map/ppermute | solution.py:403
  17.3 2.7 %first_grad.3 = f32[512,8,128]{2,1,0:T(8,128)S(1)} custom-call(bf16[896,1024]{1,0:T(8,128)(2,1)S(1)} %get-tuple-element.27.grad_out, f32[896,1024]{1,0:T(8,128)S(1)} %get-tuple-element.35.pre_hi, bf16[896,1024]{1,0:T(8,128)(2,1)S(1)} %get-tuple-element.36.inputs, bf16[1024,1024]{1,0:T(8,128)(2,1)S(1)} %copy-done), custom_call_target="tpu_custom_call" | custom-call | flops 1879048192 | bytes 8388608 | tf_op jit(solution)/shard_map/first_grad/pallas_call | solution.py:254
  20.1 1.4 %second_grad.1.keep = f32[512,8,128]{2,1,0:T(8,128)S(1)} custom-call(bf16[896,1024]{1,0:T(8,128)(2,1)S(1)} %get-tuple-element.26.act_hi, bf16[896,1024]{1,0:T(8,128)(2,1)S(1)} %get-tuple-element.27.grad_out), custom_call_target="tpu_custom_call" | custom-call | flops 939524096 | bytes 4194304 | tf_op jit(solution)/shard_map/second_grad/pallas_call | solution.py:242
  21.5 0.2 shard_map.112
  21.8 1.4 %collective-permute-start.1 = (f32[129,8,128]{2,1,0:T(8,128)S(1)}, f32[129,8,128]{2,1,0:T(8,128)S(1)}, u32[]{:S(2)}, u32[]{:S(2)}) collective-permute-start(f32[129,8,128]{2,1,0:T(8,128)S(1)} %get-tuple-element.31), channel_id=1, source_target_pairs={{0,1},{1,2},{2,3},{3,0},{4,68},{5,69},{6,70},{7,71},{8,9},{9,10},{... | collective-permute-start | bytes 1585160 | tf_op jit(solution)/shard_map/ppermute | solution.py:332
  23.2 1.5 %collective-permute-start.2 = (f32[129,8,128]{2,1,0:T(8,128)S(1)}, f32[129,8,128]{2,1,0:T(8,128)S(1)}, u32[]{:S(2)}, u32[]{:S(2)}) collective-permute-start(f32[129,8,128]{2,1,0:T(8,128)S(1)} %get-tuple-element.32), channel_id=1, source_target_pairs={{0,3},{1,0},{2,1},{3,2},{4,196},{5,197},{6,198},{7,199},{8,11},{9,... | collective-permute-start | bytes 1585160 | tf_op jit(solution)/shard_map/ppermute | solution.py:332
  24.7 2.7 %first_grad.2.keep = f32[512,8,128]{2,1,0:T(8,128)S(1)} custom-call(bf16[896,1024]{1,0:T(8,128)(2,1)S(1)} %get-tuple-element.27.grad_out, f32[896,1024]{1,0:T(8,128)S(1)} %get-tuple-element.35.pre_hi, bf16[896,1024]{1,0:T(8,128)(2,1)S(1)} %get-tuple-element.36.inputs, bf16[1024,1024]{1,0:T(8,128)(2,1)S(1)} %copy-done), custom_call_target="tpu_custom_call" | custom-call | flops 1879048192 | bytes 8388608 | tf_op jit(solution)/shard_map/first_grad/pallas_call | solution.py:254
  27.4 0.2 shard_map.115
  27.7 2.7 %collective-permute-start.7 = (f32[128,8,128]{2,1,0:T(8,128)S(1)}, f32[128,8,128]{2,1,0:T(8,128)S(1)}, u32[]{:S(2)}, u32[]{:S(2)}) collective-permute-start(f32[128,8,128]{2,1,0:T(8,128)S(1)} %get-tuple-element.39), channel_id=1, source_target_pairs={{0,3},{1,0},{2,1},{3,2},{4,196},{5,197},{6,198},{7,199},{8,11},{9,... | collective-permute-start | bytes 1572872 | tf_op jit(solution)/shard_map/ppermute | solution.py:332
  30.4 1.1 %collective-permute-done.1.came.refs_1_ = f32[129,8,128]{2,1,0:T(8,128)S(1)} collective-permute-done((f32[129,8,128]{2,1,0:T(8,128)S(1)}, f32[129,8,128]{2,1,0:T(8,128)S(1)}, u32[]{:S(2)}, u32[]{:S(2)}) %collective-permute-start.1) | collective-permute-done | bytes 528416 | tf_op jit(solution)/shard_map/ppermute | solution.py:332
  31.6 5.6 %collective-permute-done.6.came.refs_6_ = f32[128,8,128]{2,1,0:T(8,128)S(1)} collective-permute-done((f32[128,8,128]{2,1,0:T(8,128)S(1)}, f32[128,8,128]{2,1,0:T(8,128)S(1)}, u32[]{:S(2)}, u32[]{:S(2)}) %collective-permute-start.6) | collective-permute-done | bytes 524320 | tf_op jit(solution)/shard_map/ppermute | solution.py:332
  37.4 2.7 %collective-permute-start.9 = (f32[64,8,128]{2,1,0:T(8,128)S(1)}, f32[64,8,128]{2,1,0:T(8,128)S(1)}, u32[]{:S(2)}, u32[]{:S(2)}) collective-permute-start(f32[64,8,128]{2,1,0:T(8,128)S(1)} %shard_map.117), channel_id=1, source_target_pairs={{0,3},{1,0},{2,1},{3,2},{4,196},{5,197},{6,198},{7,199},{8,11},{9,... | collective-permute-start | bytes 786440 | tf_op jit(solution)/shard_map/ppermute | solution.py:332
  40.2 0.4 collective-permute-start.4
  40.6 3.2 %collective-permute-done.8.refs_8_ = f32[64,8,128]{2,1,0:T(8,128)S(1)} collective-permute-done((f32[64,8,128]{2,1,0:T(8,128)S(1)}, f32[64,8,128]{2,1,0:T(8,128)S(1)}, u32[]{:S(2)}, u32[]{:S(2)}) %collective-permute-start.8) | collective-permute-done | bytes 262176 | tf_op jit(solution)/shard_map/ppermute | solution.py:332
  43.8 2.5 %collective-permute-done.4.refs_4_ = f32[64,8,128]{2,1,0:T(8,128)S(1)} collective-permute-done((f32[64,8,128]{2,1,0:T(8,128)S(1)}, f32[64,8,128]{2,1,0:T(8,128)S(1)}, u32[]{:S(2)}, u32[]{:S(2)}) %collective-permute-start.4) | collective-permute-done | bytes 262176 | tf_op jit(solution)/shard_map/ppermute | solution.py:332
  46.3 0.2 shard_map.118
  46.5 0.9 %collective-permute-start.10 = (f32[65,8,128]{2,1,0:T(8,128)S(1)}, f32[65,8,128]{2,1,0:T(8,128)S(1)}, u32[]{:S(2)}, u32[]{:S(2)}) collective-permute-start(f32[65,8,128]{2,1,0:T(8,128)S(1)} %get-tuple-element.43), channel_id=1, source_target_pairs={{0,128},{1,129},{2,130},{3,131},{4,6},{5,7},{6,4},{7,5},{8,136},{9... | collective-permute-start | bytes 798728 | tf_op jit(solution)/shard_map/ppermute | solution.py:332
  47.4 1.8 %collective-permute-start.11 = (f32[65,8,128]{2,1,0:T(8,128)S(1)}, f32[65,8,128]{2,1,0:T(8,128)S(1)}, u32[]{:S(2)}, u32[]{:S(2)}) collective-permute-start(f32[65,8,128]{2,1,0:T(8,128)S(1)} %get-tuple-element.44), channel_id=1, source_target_pairs={{0,64},{1,65},{2,66},{3,67},{4,5},{5,6},{6,7},{7,4},{8,72},{9,73},... | collective-permute-start | bytes 798728 | tf_op jit(solution)/shard_map/ppermute | solution.py:332
  49.2 4.2 %collective-permute-done.10.b = f32[65,8,128]{2,1,0:T(8,128)S(1)} collective-permute-done((f32[65,8,128]{2,1,0:T(8,128)S(1)}, f32[65,8,128]{2,1,0:T(8,128)S(1)}, u32[]{:S(2)}, u32[]{:S(2)}) %collective-permute-start.10) | collective-permute-done | bytes 266272 | tf_op jit(solution)/shard_map/ppermute | solution.py:332
  53.4 2.2 %collective-permute-done.11.c = f32[65,8,128]{2,1,0:T(8,128)S(1)} collective-permute-done((f32[65,8,128]{2,1,0:T(8,128)S(1)}, f32[65,8,128]{2,1,0:T(8,128)S(1)}, u32[]{:S(2)}, u32[]{:S(2)}) %collective-permute-start.11) | collective-permute-done | bytes 266272 | tf_op jit(solution)/shard_map/ppermute | solution.py:332
  55.6 1.2 %collective-permute-done.12.d = f32[65,8,128]{2,1,0:T(8,128)S(1)} collective-permute-done((f32[65,8,128]{2,1,0:T(8,128)S(1)}, f32[65,8,128]{2,1,0:T(8,128)S(1)}, u32[]{:S(2)}, u32[]{:S(2)}) %collective-permute-start.12) | collective-permute-done | bytes 266272 | tf_op jit(solution)/shard_map/ppermute | solution.py:332
  56.9 25.9 %all_to_all.5.came = f32[16,5,8,128]{3,2,1,0:T(8,128)S(1)} all-to-all(f32[16,5,8,128]{3,2,1,0:T(8,128)S(1)} %bitcast.2), channel_id=1, replica_groups=mesh['dp_0'=4,'dp_1'=8,'dp_2'=2,'outer'=4] {'dp_1','dp_2'}, dimensions={0} | all-to-all | bytes 655360 | tf_op jit(solution)/shard_map/all_to_all | solution.py:418
  82.8 0.6 shard_map.120
  (18 shorter events, 0.6 us)
Async XLA Ops:
  0.6 16.7 %copy-start = (bf16[1024,1024]{1,0:T(8,128)(2,1)S(1)}, bf16[1024,1024]{1,0:T(8,128)(2,1)}, u32[]{:S(2)}) copy-start(bf16[1024,1024]{1,0:T(8,128)(2,1)} %w2.5) | copy-start | bytes 6291460
  16.4 5.1 %collective-permute-start = (f32[513,8,128]{2,1,0:T(8,128)S(1)}, f32[513,8,128]{2,1,0:T(8,128)S(1)}, u32[]{:S(2)}, u32[]{:S(2)}) collective-permute-start(f32[513,8,128]{2,1,0:T(8,128)S(1)} %get-tuple-element.28), channel_id=1, source_target_pairs={{0,4},{4,0},{1,5},{5,1},{2,6},{6,2},{3,7},{7,3},{8,12},{12,8},{9,1... | collective-permute-start | bytes 6303752 | tf_op jit(solution)/shard_map/ppermute | solution.py:403
  20.0 7.3 %collective-permute-start.5 = (f32[512,8,128]{2,1,0:T(8,128)S(1)}, f32[512,8,128]{2,1,0:T(8,128)S(1)}, u32[]{:S(2)}, u32[]{:S(2)}) collective-permute-start(f32[512,8,128]{2,1,0:T(8,128)S(1)} %first_grad.3), channel_id=1, source_target_pairs={{0,4},{4,0},{1,5},{5,1},{2,6},{6,2},{3,7},{7,3},{8,12},{12,8},{9,1... | collective-permute-start | bytes 6291464 | tf_op jit(solution)/shard_map/ppermute | solution.py:403
  21.8 9.7 %collective-permute-start.1 = (f32[129,8,128]{2,1,0:T(8,128)S(1)}, f32[129,8,128]{2,1,0:T(8,128)S(1)}, u32[]{:S(2)}, u32[]{:S(2)}) collective-permute-start(f32[129,8,128]{2,1,0:T(8,128)S(1)} %get-tuple-element.31), channel_id=1, source_target_pairs={{0,1},{1,2},{2,3},{3,0},{4,68},{5,69},{6,70},{7,71},{8,9},{9,10},{... | collective-permute-start | bytes 1585160 | tf_op jit(solution)/shard_map/ppermute | solution.py:332
  23.2 17.0 %collective-permute-start.2 = (f32[129,8,128]{2,1,0:T(8,128)S(1)}, f32[129,8,128]{2,1,0:T(8,128)S(1)}, u32[]{:S(2)}, u32[]{:S(2)}) collective-permute-start(f32[129,8,128]{2,1,0:T(8,128)S(1)} %get-tuple-element.32), channel_id=1, source_target_pairs={{0,3},{1,0},{2,1},{3,2},{4,196},{5,197},{6,198},{7,199},{8,11},{9,... | collective-permute-start | bytes 1585160 | tf_op jit(solution)/shard_map/ppermute | solution.py:332
  27.6 9.6 %collective-permute-start.6 = (f32[128,8,128]{2,1,0:T(8,128)S(1)}, f32[128,8,128]{2,1,0:T(8,128)S(1)}, u32[]{:S(2)}, u32[]{:S(2)}) collective-permute-start(f32[128,8,128]{2,1,0:T(8,128)S(1)} %get-tuple-element.38), channel_id=1, source_target_pairs={{0,1},{1,2},{2,3},{3,0},{4,68},{5,69},{6,70},{7,71},{8,9},{9,10},{... | collective-permute-start | bytes 1572872 | tf_op jit(solution)/shard_map/ppermute | solution.py:332
  27.7 9.6 %collective-permute-start.7 = (f32[128,8,128]{2,1,0:T(8,128)S(1)}, f32[128,8,128]{2,1,0:T(8,128)S(1)}, u32[]{:S(2)}, u32[]{:S(2)}) collective-permute-start(f32[128,8,128]{2,1,0:T(8,128)S(1)} %get-tuple-element.39), channel_id=1, source_target_pairs={{0,3},{1,0},{2,1},{3,2},{4,196},{5,197},{6,198},{7,199},{8,11},{9,... | collective-permute-start | bytes 1572872 | tf_op jit(solution)/shard_map/ppermute | solution.py:332
  31.5 14.7 %collective-permute-start.3 = (f32[65,8,128]{2,1,0:T(8,128)S(1)}, f32[65,8,128]{2,1,0:T(8,128)S(1)}, u32[]{:S(2)}, u32[]{:S(2)}) collective-permute-start(f32[65,8,128]{2,1,0:T(8,128)S(1)} %shard_map.113), channel_id=1, source_target_pairs={{0,1},{1,2},{2,3},{3,0},{4,68},{5,69},{6,70},{7,71},{8,9},{9,10},{... | collective-permute-start | bytes 798728 | tf_op jit(solution)/shard_map/ppermute | solution.py:332
  37.3 6.5 %collective-permute-start.8 = (f32[64,8,128]{2,1,0:T(8,128)S(1)}, f32[64,8,128]{2,1,0:T(8,128)S(1)}, u32[]{:S(2)}, u32[]{:S(2)}) collective-permute-start(f32[64,8,128]{2,1,0:T(8,128)S(1)} %shard_map.116), channel_id=1, source_target_pairs={{0,1},{1,2},{2,3},{3,0},{4,68},{5,69},{6,70},{7,71},{8,9},{9,10},{... | collective-permute-start | bytes 786440 | tf_op jit(solution)/shard_map/ppermute | solution.py:332
  37.4 6.4 %collective-permute-start.9 = (f32[64,8,128]{2,1,0:T(8,128)S(1)}, f32[64,8,128]{2,1,0:T(8,128)S(1)}, u32[]{:S(2)}, u32[]{:S(2)}) collective-permute-start(f32[64,8,128]{2,1,0:T(8,128)S(1)} %shard_map.117), channel_id=1, source_target_pairs={{0,3},{1,0},{2,1},{3,2},{4,196},{5,197},{6,198},{7,199},{8,11},{9,... | collective-permute-start | bytes 786440 | tf_op jit(solution)/shard_map/ppermute | solution.py:332
  40.2 6.1 %collective-permute-start.4 = (f32[64,8,128]{2,1,0:T(8,128)S(1)}, f32[64,8,128]{2,1,0:T(8,128)S(1)}, u32[]{:S(2)}, u32[]{:S(2)}) collective-permute-start(f32[64,8,128]{2,1,0:T(8,128)S(1)} %shard_map.114), channel_id=1, source_target_pairs={{0,3},{1,0},{2,1},{3,2},{4,196},{5,197},{6,198},{7,199},{8,11},{9,... | collective-permute-start | bytes 786440 | tf_op jit(solution)/shard_map/ppermute | solution.py:332
  46.5 7.0 %collective-permute-start.10 = (f32[65,8,128]{2,1,0:T(8,128)S(1)}, f32[65,8,128]{2,1,0:T(8,128)S(1)}, u32[]{:S(2)}, u32[]{:S(2)}) collective-permute-start(f32[65,8,128]{2,1,0:T(8,128)S(1)} %get-tuple-element.43), channel_id=1, source_target_pairs={{0,128},{1,129},{2,130},{3,131},{4,6},{5,7},{6,4},{7,5},{8,136},{9... | collective-permute-start | bytes 798728 | tf_op jit(solution)/shard_map/ppermute | solution.py:332
  47.4 8.2 %collective-permute-start.11 = (f32[65,8,128]{2,1,0:T(8,128)S(1)}, f32[65,8,128]{2,1,0:T(8,128)S(1)}, u32[]{:S(2)}, u32[]{:S(2)}) collective-permute-start(f32[65,8,128]{2,1,0:T(8,128)S(1)} %get-tuple-element.44), channel_id=1, source_target_pairs={{0,64},{1,65},{2,66},{3,67},{4,5},{5,6},{6,7},{7,4},{8,72},{9,73},... | collective-permute-start | bytes 798728 | tf_op jit(solution)/shard_map/ppermute | solution.py:332
  49.2 7.6 %collective-permute-start.12 = (f32[65,8,128]{2,1,0:T(8,128)S(1)}, f32[65,8,128]{2,1,0:T(8,128)S(1)}, u32[]{:S(2)}, u32[]{:S(2)}) collective-permute-start(f32[65,8,128]{2,1,0:T(8,128)S(1)} %get-tuple-element.45), channel_id=1, source_target_pairs={{0,192},{1,193},{2,194},{3,195},{4,7},{5,4},{6,5},{7,6},{8,200},{9... | collective-permute-start | bytes 798728 | tf_op jit(solution)/shard_map/ppermute | solution.py:332
